TPU v7x, 32 devices: a whole 2x2x4 slice. The times are simulated.
32 devices in a mesh: ens: 16 (over z, y, core), batch: 2 (over x).
Axes of the slice: x: 2, y: 2, z: 4, core: 2. Of those that a mesh axis runs over, the one named last changes fastest.
Arguments:
- replay_obs: bfloat16 [512, 1024], P('batch'), may hold values from -4.1875 to 4.1875
- replay_next: bfloat16 [512, 1024], P('batch'), may hold values from -4.1875 to 4.1875
- batch_rows: int32 [64], P('batch'), may hold values from 0 to 255
- data_action: int32 [64], P('batch'), may hold values from 0 to 255
- next_action: int32 [64], P('batch'), may hold values from 0 to 255
- sampled_actions: int32 [64, 16], P('batch'), may hold values from 0 to 255
- reward: float32 [64], P('batch'), may hold values from -6 to 6
- next_logp: float32 [64], P('batch'), may hold values from -6 to 2
- action_table: bfloat16 [256, 1024], replicated, may hold values from -4.1875 to 4.1875
- w1: bfloat16 [16, 4096, 1024], P('ens'), may hold values from -0.1875 to 0.1875
- w2: float32 [16, 4096], P('ens'), may hold values from -0.375 to 0.375
Outputs:
- grad_w1: float32 [16, 4096, 1024], P('ens', 'batch')
- grad_w2: float32 [16, 4096], P('ens')
- critic_stats: float32 [16, 3], P('ens')
Inputs may be any that keep to these rules, and one draw needn't show every extreme that they name: `batch_rows`: each entry is a row of the own block of 256 replay rows that holds its state.
All inputs are finite; a program needn't handle non-finite values.
Results may differ from a plain program's by a relative error of at most 0.0045.
Values may be sent and summed in bfloat16 or wider, within the bound.
A program may use at most 128 MiB of HBM per device.

v0:
```python
import functools

import jax
import jax.numpy as jnp
from jax import lax
from jax.experimental import pallas as pl
from jax.experimental.pallas import tpu as pltpu
from jax.sharding import PartitionSpec as P

discount = 0.99
entropy_temp = 0.2
penalty_weight = 1.0
diversity_weight = 1000.0

MESH = pl.DeviceIdType.MESH
F32 = jnp.float32
BF16 = jnp.bfloat16
CHUNK = 256
LANES = 128


def dot_t(a, b):
    return lax.dot_general(a, b, (((1,), (1,)), ((), ())), preferred_element_type=F32)


def sigmoid(x):
    return 0.5 * jnp.tanh(0.5 * x) + 0.5


def kernel(
    n_ens, per_dev, samples, critics_total,
    obs_ref, next_ref, rows_ref, next_act_ref, data_act_ref, samp_act_ref, reward_ref, logp_ref, table_ref, w2_ref, w1_ref,
    lhs_ref, rhs_ref, gv_ref, stat_ref,
    acts_ref, aux_ref, wbuf, xall, acts_in, aux_in, sel, sel_dq, ptab, pbuf, base, pre0, dbuf, cbuf, vb, sbuf, ubuf,
    gpart, gsend, grecv, qpart, qrecv, unit, usend, urecv, qmine, qall, spread_mine, spread_all,
    dgrad, div_out, div_in, gsamp, gvsamp, gvbuf,
    w_sem, a_send, a_recv, g_send, g_recv, u_send, u_recv, m_send, m_recv, s_send, s_recv,
    d_send, d_recv, v_send, v_recv,
):
    e = lax.axis_index("ens")
    b = lax.axis_index("batch")
    peer = 1 - b
    states = 2 * per_dev
    block = 2 * states
    nact = table_ref.shape[0]
    width = table_ref.shape[1]
    cols = acts_ref.shape[1]
    samp_cols = cols - block
    half = wbuf.shape[0]
    chunks = half // CHUNK
    pair = {"ens": e, "batch": peer}

    def other(k):
        return {"ens": lax.rem(e + k, n_ens), "batch": b}

    barrier = pltpu.get_barrier_semaphore()
    pl.semaphore_signal(barrier, inc=1, device_id=pair, device_id_type=MESH)

    def greet(k, carry):
        pl.semaphore_signal(barrier, inc=1, device_id=other(k), device_id_type=MESH)
        return carry

    lax.fori_loop(1, n_ens, greet, 0)

    def w_copy(c):
        return pltpu.make_async_copy(
            w1_ref.at[0, pl.ds(b * half + c * CHUNK, CHUNK), :],
            wbuf.at[pl.ds(c * CHUNK, CHUNK), :],
            w_sem.at[c],
        )

    for c in range(chunks):
        w_copy(c).start()

    own_rows = pl.ds(pl.multiple_of(b * per_dev, per_dev), per_dev)
    peer_rows = pl.ds(pl.multiple_of(peer * per_dev, per_dev), per_dev)
    buf_rows = obs_ref.shape[0]
    row = jnp.concatenate([rows_ref[...], jnp.zeros((1, LANES - per_dev), jnp.int32)], axis=1)
    pick = row == lax.broadcasted_iota(jnp.int32, (buf_rows, LANES), 0)
    pick = jnp.transpose(jnp.where(pick, 1.0, 0.0))[:per_dev, :].astype(BF16)
    xall[0, own_rows, :] = jnp.dot(pick, next_ref[...], preferred_element_type=F32).astype(BF16)
    xall[1, own_rows, :] = jnp.dot(pick, obs_ref[...], preferred_element_type=F32).astype(BF16)
    act_rows = [next_act_ref[...], data_act_ref[...]]
    act_rows += [samp_act_ref[i:i + 1, :] for i in range(samples)]

    def place(part):
        return [jnp.where(b == 0, part, jnp.zeros_like(part)), jnp.where(b == 0, jnp.zeros_like(part), part)]

    for j in range(cols // block):
        acts_ref[:, j * block:(j + 1) * block] = jnp.concatenate(
            place(act_rows[2 * j]) + place(act_rows[2 * j + 1]), axis=1
        )
    blank = jnp.zeros((1, states), F32)
    aux_ref[0:1, :] = jnp.concatenate([blank] + place(reward_ref[...]), axis=1)
    aux_ref[1:2, :] = jnp.concatenate([blank] + place(logp_ref[...]), axis=1)
    pl.semaphore_wait(barrier, n_ens)

    def remote(src, dst, send, recv, to):
        return pltpu.make_async_remote_copy(
            src_ref=src, dst_ref=dst, send_sem=send, recv_sem=recv,
            device_id=to, device_id_type=MESH,
        )

    first = [
        remote(xall.at[:, own_rows, :], xall.at[:, own_rows, :], a_send.at[0], a_recv.at[0], pair),
        remote(acts_ref, acts_in, a_send.at[1], a_recv.at[1], pair),
        remote(aux_ref, aux_in, a_send.at[2], a_recv.at[2], pair),
    ]
    for copy in first:
        copy.start()

    def table_step(c, carry):
        rows = pl.ds(pl.multiple_of(c * CHUNK, CHUNK), CHUNK)
        w_copy(c).wait()
        ptab[rows, :] = dot_t(wbuf[rows, :], table_ref[...]).astype(BF16)
        v_row = w2_ref[0:1, pl.ds(pl.multiple_of(b * half + c * CHUNK, CHUNK), CHUNK)]
        vb[rows, :] = jnp.transpose(jnp.broadcast_to(v_row, (LANES, CHUNK)))
        return carry

    lax.fori_loop(0, chunks, table_step, 0)

    for copy in first:
        copy.wait()
    acts = acts_ref[...] + acts_in[...]
    lane_all = lax.broadcasted_iota(jnp.int32, (1, cols), 1)
    state_row = jnp.where(lane_all >= states, nact + lax.rem(lane_all, states), -1)
    for j in range(cols // LANES):
        at = slice(j * LANES, (j + 1) * LANES)
        row = lax.broadcasted_iota(jnp.int32, (nact + block, LANES), 0)
        hit = jnp.logical_or(row == acts[:, at], row == state_row[:, at])
        sel[:, at] = jnp.where(hit, 1.0, 0.0).astype(BF16)

    lane = lax.broadcasted_iota(jnp.int32, (1, block), 1)
    low = lane < states
    gpart[...] = jnp.zeros_like(gpart)
    SUB = 32

    def data_forward(c, q_acc):
        rows = pl.ds(pl.multiple_of(c * CHUNK, CHUNK), CHUNK)
        w = wbuf[rows, :]
        x = jnp.concatenate([xall[0], xall[1]], axis=0)
        p0 = dot_t(w, x)
        pre = p0 + jnp.dot(ptab[rows, :], sel[:nact, :block], preferred_element_type=F32)
        pre0[rows, :] = pre
        base[rows, :] = jnp.where(low, pltpu.roll(p0, states, 1), p0)
        v = vb[rows, :]
        sig = sigmoid(pre)
        silu = pre * sig
        slope = sig * (1.0 + (pre - silu))
        co = jnp.transpose(v * slope)[states:, :].astype(BF16)
        gpart[...] += jnp.dot(co, w, preferred_element_type=F32)
        return q_acc + jnp.sum(silu * v, axis=0, keepdims=True)

    qpart[:, :block] = lax.fori_loop(0, chunks, data_forward, jnp.zeros((1, block), F32))
    gsend[...] = gpart[peer_rows, :].astype(gsend.dtype)
    second = [
        remote(qpart.at[:, :block], qrecv.at[:, :block], g_send.at[0], g_recv.at[0], pair),
        remote(gsend, grecv, g_send.at[1], g_recv.at[1], pair),
        remote(qpart.at[:, block:], qrecv.at[:, block:], g_send.at[2], g_recv.at[2], pair),
    ]
    second[0].start()
    second[1].start()

    def samp_forward(c, q_acc):
        rows = pl.ds(pl.multiple_of(c * CHUNK, CHUNK), CHUNK)
        pbuf[...] = jnp.dot(ptab[rows, :], sel[:nact, block:], preferred_element_type=F32)

        def sub_step(r, acc):
            here = pl.ds(pl.multiple_of(r * SUB, SUB), SUB)
            there = pl.ds(pl.multiple_of(c * CHUNK + r * SUB, SUB), SUB)
            v = vb[there, :]
            start = base[there, :]
            out = []
            for j in range(samp_cols // LANES):
                at = slice(j * LANES, (j + 1) * LANES)
                pre = pbuf[here, at] + start
                sig = sigmoid(pre)
                silu = pre * sig
                slope = sig * (1.0 + (pre - silu))
                sbuf[there, at] = (v * slope).astype(BF16)
                ubuf[there, at] = silu.astype(BF16)
                sv = silu * v
                part = sv[0:8]
                for t in range(1, SUB // 8):
                    part = part + sv[8 * t:8 * t + 8]
                out.append(acc[j] + part)
            return tuple(out)

        return lax.fori_loop(0, CHUNK // SUB, sub_step, q_acc)

    q_acc = (jnp.zeros((8, LANES), F32),) * (samp_cols // LANES)
    cut_one, cut_two = (3 * chunks) // 8, (6 * chunks) // 8
    q_acc = lax.fori_loop(0, cut_one, samp_forward, q_acc)
    second[0].wait()
    q0 = qpart[:, :block] + qrecv[:, :block]
    qmine[...] = jnp.broadcast_to(q0, qmine.shape)

    def q_copy(k):
        return remote(qmine, qall.at[k], m_send.at[k], m_recv.at[k], other(k))

    def u_copy(k):
        return remote(
            usend.at[lax.rem(e + k, n_ens)], urecv.at[k], u_send.at[k], u_recv.at[k], other(k)
        )

    def s_copy(k):
        return remote(spread_mine, spread_all.at[e], s_send.at[k], s_recv.at[k], other(k))

    def start_all(make):
        def go(k, carry):
            make(k).start()
            return carry
        lax.fori_loop(1, n_ens, go, 0)

    def wait_all(make):
        def go(k, carry):
            make(k).wait()
            return carry
        lax.fori_loop(1, n_ens, go, 0)

    start_all(q_copy)
    second[1].wait()
    grad_in = gpart[own_rows, :] + grecv[...].astype(F32)
    norm_sq = jnp.sum(grad_in * grad_in, axis=-1, keepdims=True) + 1.0
    in_norm = jnp.sqrt(norm_sq)
    unit[...] = grad_in / in_norm
    piece = usend.shape[1]
    per_col = per_dev // piece
    for p in range(n_ens):
        c0, r0 = p // per_col, (p % per_col) * piece
        usend[p] = unit[r0:r0 + piece, c0 * LANES:(c0 + 1) * LANES].astype(BF16)
    start_all(u_copy)

    q_acc = lax.fori_loop(cut_one, cut_two, samp_forward, q_acc)

    wait_all(u_copy)
    total = usend[e].astype(F32)
    for k in range(1, n_ens):
        total = total + urecv[k].astype(F32)
    spread_mine[...] = total.astype(BF16)
    spread_all[e] = total.astype(BF16)
    start_all(s_copy)
    q_acc = lax.fori_loop(cut_two, chunks, samp_forward, q_acc)
    for j in range(samp_cols // LANES):
        qpart[:, block + j * LANES:block + (j + 1) * LANES] = jnp.sum(q_acc[j], axis=0, keepdims=True)
    second[2].start()
    wait_all(q_copy)
    floor = qmine[...]
    for k in range(1, n_ens):
        floor = jnp.minimum(floor, qall[k])
    floor = pltpu.roll(floor, states, 1)[0:1, :]
    aux = aux_ref[...] + aux_in[...]
    target = aux[0:1, :] + discount * (floor - entropy_temp * aux[1:2, :])
    td_gap = q0 - target
    dq_data = jnp.where(low, 0.0, (2.0 * td_gap - penalty_weight) / states)

    wait_all(s_copy)
    scale = 2.0 * diversity_weight / (critics_total - 1) / states
    for p in range(n_ens):
        c0, r0 = p // per_col, (p % per_col) * piece
        gpart[r0:r0 + piece, c0 * LANES:(c0 + 1) * LANES] = spread_all[p].astype(F32)
    unit_dir = unit[...]
    away = gpart[:per_dev, :] - unit_dir
    div_row = jnp.sum(unit_dir * away, axis=-1, keepdims=True)
    dg = scale * (away - unit_dir * div_row) / in_norm
    dg_rows = pl.ds(pl.multiple_of(states + b * per_dev, per_dev), per_dev)
    dgrad[:states, :] = jnp.zeros((states, width), BF16)
    dgrad[dg_rows, :] = dg.astype(BF16)
    div_sum = jnp.sum(div_row, axis=0, keepdims=True)
    div_out[...] = jnp.broadcast_to(div_sum, div_out.shape)
    third = [
        remote(dgrad.at[dg_rows, :], dgrad.at[dg_rows, :], d_send.at[0], d_recv.at[0], pair),
        remote(div_out, div_in, d_send.at[1], d_recv.at[1], pair),
    ]
    for copy in third:
        copy.start()
    second[2].wait()
    q_samp = qpart[:, block:] + qrecv[:, block:]
    exps = jnp.exp(q_samp)
    mass = exps[:, :block]
    for j in range(1, (cols - block) // block):
        mass = mass + exps[:, j * block:(j + 1) * block]
    mass = mass + pltpu.roll(mass, states, 1)
    log_mass = jnp.log(mass)
    tiled = jnp.concatenate([log_mass] * ((cols - block) // block), axis=1)
    dq_samp = penalty_weight * jnp.exp(q_samp - tiled) / states
    for j in range((cols - block) // LANES):
        at = slice(j * LANES, (j + 1) * LANES)
        src = slice(block + j * LANES, block + (j + 1) * LANES)
        sel_dq[:, at] = (sel[:, src].astype(F32) * dq_samp[:, at]).astype(BF16)

    def samp_step(c, carry):
        rows = pl.ds(pl.multiple_of(c * CHUNK, CHUNK), CHUNK)
        gsamp[rows, :] = dot_t(sbuf[rows, :], sel_dq[...])

        def sub_step(r, inner):
            there = pl.ds(pl.multiple_of(c * CHUNK + r * SUB, SUB), SUB)
            total = ubuf[there, :LANES].astype(F32) * dq_samp[:, :LANES]
            for j in range(1, (cols - block) // LANES):
                at = slice(j * LANES, (j + 1) * LANES)
                total = total + ubuf[there, at].astype(F32) * dq_samp[:, at]
            gvsamp[there, :] = total
            return inner

        lax.fori_loop(0, CHUNK // SUB, sub_step, 0)
        return carry

    lax.fori_loop(0, chunks, samp_step, 0)
    rhs_ref[:nact, :] = table_ref[...]
    rhs_ref[nact:nact + states, :] = xall[1]
    for copy in third:
        copy.wait()
    rhs_ref[nact + states:, :] = dgrad[states:, :]

    td_total = jnp.sum(jnp.where(low, 0.0, td_gap * td_gap), axis=1, keepdims=True)
    gap_total = jnp.sum(jnp.where(low, 0.0, log_mass - q0), axis=1, keepdims=True)
    div_total = div_out[0:1, :] + div_in[0:1, :]
    stats = jnp.where(lane == 0, td_total, jnp.where(lane == 1, gap_total, div_total))
    stat_ref[...] = (stats / states)[:, :3]

    def data_step(c, carry):
        rows = pl.ds(pl.multiple_of(c * CHUNK, CHUNK), CHUNK)
        dcoef = dot_t(wbuf[rows, :], dgrad[...])
        pre = pre0[rows, :]
        v = vb[rows, :]
        sig = sigmoid(pre)
        silu = pre * sig
        slope = sig * (1.0 + (pre - silu))
        curve = sig * (1.0 - sig) * (2.0 + pre * (1.0 - 2.0 * sig))
        dpre = (v * (dq_data * slope + dcoef * curve)).astype(BF16)
        coeff = jnp.where(low, 0.0, v * slope)
        dbuf[rows, :] = dpre
        cbuf[rows, :] = coeff
        gv = gvsamp[rows, :] + dq_data * silu + dcoef * slope
        gvbuf[b, pl.ds(c, 1), :] = jnp.sum(jnp.transpose(gv), axis=0, keepdims=True)
        return carry

    lax.fori_loop(0, chunks, data_step, 0)
    last = remote(gvbuf.at[b], gvbuf.at[b], v_send, v_recv, pair)
    last.start()

    def out_step(c, carry):
        rows = pl.ds(pl.multiple_of(c * CHUNK, CHUNK), CHUNK)
        grads = gsamp[rows, :] + dot_t(dbuf[rows, :], sel[:, :block])
        lhs_ref[rows, :nact] = grads[:, :nact].astype(BF16)
        lhs_ref[rows, nact:] = (grads[:, nact:] + cbuf[rows, :]).astype(BF16)
        return carry

    lax.fori_loop(0, chunks, out_step, 0)
    last.wait()
    for i in range(2):
        for c in range(chunks):
            at = i * half + c * CHUNK
            gv_ref[:, at:at + CHUNK] = gvbuf[i, c:c + 1, :]


def body(
    replay_obs, replay_next, batch_rows, data_action, next_action, sampled_actions,
    reward, next_logp, action_table, w1, w2,
):
    per_dev = batch_rows.shape[0]
    samples = sampled_actions.shape[1]
    width = replay_obs.shape[1]
    hidden = w1.shape[1]
    n_batch = lax.axis_size("batch")
    n_ens = lax.axis_size("ens")
    if n_batch != 2 or w1.shape[0] != 1:
        raise ValueError("unsupported mesh")
    states = per_dev * n_batch
    block = 2 * states
    half = hidden // n_batch
    nact = action_table.shape[0]
    cols = (samples + 2) * states
    chunks = half // CHUNK
    piece = per_dev * width // LANES // n_ens
    vmem = pl.BlockSpec(memory_space=pltpu.VMEM)
    dma = pltpu.SemaphoreType.DMA
    lhs, rhs, gv, stats = pl.pallas_call(
        functools.partial(kernel, n_ens, per_dev, samples, n_ens * w1.shape[0]),
        out_shape=(
            jax.ShapeDtypeStruct((half, nact + block), BF16),
            jax.ShapeDtypeStruct((nact + block, width), BF16),
            jax.ShapeDtypeStruct((1, hidden), F32),
            jax.ShapeDtypeStruct((1, 3), F32),
        ),
        in_specs=[vmem] * 10 + [pl.BlockSpec(memory_space=pl.ANY)],
        out_specs=(vmem,) * 4,
        scratch_shapes=[
            pltpu.VMEM((1, cols), jnp.int32),
            pltpu.VMEM((2, block), F32),
            pltpu.VMEM((half, width), BF16),
            pltpu.VMEM((2, states, width), BF16),
            pltpu.VMEM((1, cols), jnp.int32),
            pltpu.VMEM((2, block), F32),
            pltpu.VMEM((nact + block, cols), BF16),
            pltpu.VMEM((nact + block, cols - block), BF16),
            pltpu.VMEM((half, nact), BF16),
            pltpu.VMEM((CHUNK, cols - block), F32),
            pltpu.VMEM((half, block), F32),
            pltpu.VMEM((half, block), F32),
            pltpu.VMEM((half, block), BF16),
            pltpu.VMEM((half, block), F32),
            pltpu.VMEM((half, LANES), F32),
            pltpu.VMEM((half, cols - block), BF16),
            pltpu.VMEM((half, cols - block), BF16),
            pltpu.VMEM((states, width), F32),
            pltpu.VMEM((per_dev, width), BF16),
            pltpu.VMEM((per_dev, width), BF16),
            pltpu.VMEM((1, cols), F32),
            pltpu.VMEM((1, cols), F32),
            pltpu.VMEM((per_dev, width), F32),
            pltpu.VMEM((n_ens, piece, LANES), BF16),
            pltpu.VMEM((n_ens, piece, LANES), BF16),
            pltpu.VMEM((8, block), F32),
            pltpu.VMEM((n_ens, 8, block), F32),
            pltpu.VMEM((piece, LANES), BF16),
            pltpu.VMEM((n_ens, piece, LANES), BF16),
            pltpu.VMEM((block, width), BF16),
            pltpu.VMEM((8, block), F32),
            pltpu.VMEM((8, block), F32),
            pltpu.VMEM((half, nact + block), F32),
            pltpu.VMEM((half, LANES), F32),
            pltpu.VMEM((2, chunks, CHUNK), F32),
            dma((chunks,)),
            dma((3,)), dma((3,)), dma((3,)), dma((3,)),
            dma((n_ens,)), dma((n_ens,)), dma((n_ens,)), dma((n_ens,)), dma((n_ens,)), dma((n_ens,)),
            dma((2,)), dma((2,)), dma, dma,
        ],
        compiler_params=pltpu.CompilerParams(
            collective_id=0, has_side_effects=True, vmem_limit_bytes=60 * 1024 * 1024
        ),
    )(
        replay_obs, replay_next, batch_rows[None], next_action[None], data_action[None],
        sampled_actions.T, reward[None], next_logp[None], action_table, w2, w1,
    )
    grad_w1 = jnp.dot(lhs, rhs, preferred_element_type=F32)[None]
    return (grad_w1, gv, stats)


def solution(mesh):
    return jax.shard_map(
        body,
        mesh=mesh,
        in_specs=(
            P("batch", None),
            P("batch", None),
            P("batch"),
            P("batch"),
            P("batch"),
            P("batch", None),
            P("batch"),
            P("batch"),
            P(),
            P("ens", None, None),
            P("ens", None),
        ),
        out_specs=(P("ens", "batch", None), P("ens", None), P("ens", None)),
        check_vma=False,
    )
```

profile of v0, /device:TPU:0, one launch (start us, length us, event | category | flops | bytes accessed | tf_op | source)
XLA Modules:
  0.0 53.8 jit_solution(15180374334329083208)
XLA Ops:
  0.6 44.6 %shard_map.130 = (bf16[2048,384]{1,0:T(8,128)(2,1)}, bf16[384,1024]{1,0:T(8,128)(2,1)}, f32[1,4096]{1,0:T(1,128)}, f32[1,3]{1,0:T(1,128)}) custom-call(bf16[256,1024]{1,0:T(8,128)(2,1)} %obs_ref.1, bf16[256,1024]{1,0:T(8,128)(2,1)} %next_ref.1, s32[1,32]{1,0:T(1,128)} %bitcast.11, s32[1,32]{1,0:T(1,128)} %bitcast.12, s32[1,32]{1,0:T(1,128)} %bitcast.13, ...), custom_call_target="tpu_custom_call" | custom-call | tf_op jit(solution)/shard_map/pallas_call | solution.py:378
  45.3 0.0 copy-start
  45.3 0.0 copy-start.1
  45.3 7.3 %convolution_bitcast_fusion = f32[1,2048,1024]{2,1,0:T(8,128)} fusion(bf16[2048,384]{1,0:T(8,128)(2,1)} %get-tuple-element.7, bf16[384,1024]{1,0:T(8,128)(2,1)} %get-tuple-element.8), kind=kOutput, calls=%fused_computation | convolution fusion | flops 1610612736 | bytes 10747904 | tf_op jit(solution)/shard_map/dot_general | solution.py:436
  52.7 0.0 copy-done
  52.7 0.6 %copy.16 = f32[1,4096]{1,0:T(1,128)} copy(f32[1,4096]{1,0:T(1,128)S(1)} %copy-done) | data formatting | bytes 32768
  53.3 0.0 copy-done.1
  53.3 0.5 copy.17
Async XLA Ops:
  45.3 7.4 %copy-start = (f32[1,4096]{1,0:T(1,128)S(1)}, f32[1,4096]{1,0:T(1,128)}, u32[]{:S(2)}) copy-start(f32[1,4096]{1,0:T(1,128)} %get-tuple-element.15) | copy-start | bytes 49156
  45.3 8.0 %copy-start.1 = (f32[1,3]{1,0:T(1,128)S(1)}, f32[1,3]{1,0:T(1,128)}, u32[]{:S(2)}) copy-start(f32[1,3]{1,0:T(1,128)} %get-tuple-element.16) | copy-start | bytes 40
where the time goes:
time: 54 us; the launch traced here: 53.8 us
  Pallas kernels  44.6 us (83%)
  matrix products  7.35 us (14%)
  local copies, waits for them, and re-layouts  1.12 us (2%)
  between operations  0.66 us (1%)
    pallas_call x1, Pallas kernels, body(): pl.pallas_call(functools.partial(kernel, n_ens, per_dev, samples, n_ens *...  44.6 us
    dot_general x1, matrix products, body(): grad_w1 = jnp.dot(lhs, rhs, preferred_element_type=F32)[None]  7.35 us
    unnamed x6, local copies, waits for them, and re-layouts  1.12 us

commit v1 on v0

v1 whole, which is shorter than its diff:
```python
import functools

import jax
import jax.numpy as jnp
from jax import lax
from jax.experimental import pallas as pl
from jax.experimental.pallas import tpu as pltpu
from jax.sharding import PartitionSpec as P

discount = 0.99
entropy_temp = 0.2
penalty_weight = 1.0
diversity_weight = 1000.0

MESH = pl.DeviceIdType.MESH
F32 = jnp.float32
BF16 = jnp.bfloat16
CHUNK = 256
LANES = 128
VMEM_LIMIT = 60 * 1024 * 1024
VMEM_LIMIT_2 = 60 * 1024 * 1024


def dot_t(a, b):
    return lax.dot_general(a, b, (((1,), (1,)), ((), ())), preferred_element_type=F32)


def sigmoid(x):
    return 0.5 * jnp.tanh(0.5 * x) + 0.5


def kernel(
    n_ens, per_dev, samples, critics_total,
    rows_ref, next_act_ref, data_act_ref, samp_act_ref, reward_ref, logp_ref, w2_ref,
    obs_hbm, next_hbm, table_hbm, w1_ref,
    lhs_hbm, rhs_hbm, gv_ref, stat_ref,
    obs_ref, next_ref, table_ref, acts_ref, aux_ref, wbuf, xcat, xnext, acts_in, aux_in, sel, sel_dq, ptab,
    pbuf_a, pbuf_b, base, pcat, vb, cot, sbuf, ubuf,
    gpart, gsend, grecv, qpart, qrecv, unit, usend, urecv, qmine, qall, spread_mine, spread_all,
    dgrad, div_out, div_in, dcoef_buf, gvsamp, gvbuf, lhs, tabd,
    in_sem, w_sem, a_send, a_recv, g_send, g_recv, u_send, u_recv, m_send, m_recv, s_send, s_recv,
    d_send, d_recv, v_send, v_recv, o_sem,
):
    e = lax.axis_index("ens")
    b = lax.axis_index("batch")
    peer = 1 - b
    states = 2 * per_dev
    block = 2 * states
    nact = table_ref.shape[0]
    width = table_ref.shape[1]
    cols = acts_ref.shape[1]
    samp_cols = cols - block
    groups = samp_cols // LANES
    half = wbuf.shape[0]
    chunks = half // CHUNK
    pair = {"ens": e, "batch": peer}

    def other(k):
        return {"ens": lax.rem(e + k, n_ens), "batch": b}

    barrier = pltpu.get_barrier_semaphore()
    pl.semaphore_signal(barrier, inc=1, device_id=pair, device_id_type=MESH)

    def greet(k, carry):
        pl.semaphore_signal(barrier, inc=1, device_id=other(k), device_id_type=MESH)
        return carry

    lax.fori_loop(1, n_ens, greet, 0)

    loads = [
        pltpu.make_async_copy(obs_hbm, obs_ref, in_sem.at[0]),
        pltpu.make_async_copy(table_hbm, table_ref, in_sem.at[1]),
        pltpu.make_async_copy(next_hbm, next_ref, in_sem.at[2]),
    ]
    for copy in loads:
        copy.start()

    def w_copy(c):
        return pltpu.make_async_copy(
            w1_ref.at[0, pl.ds(b * half + c * CHUNK, CHUNK), :],
            wbuf.at[pl.ds(c * CHUNK, CHUNK), :],
            w_sem.at[c],
        )

    for c in range(chunks):
        w_copy(c).start()

    own_rows = pl.ds(pl.multiple_of(b * per_dev, per_dev), per_dev)
    peer_rows = pl.ds(pl.multiple_of(peer * per_dev, per_dev), per_dev)

    def one_hot(index_row, length):
        row = jnp.concatenate([index_row, jnp.zeros((1, LANES - per_dev), jnp.int32)], axis=1)
        hit = row == lax.broadcasted_iota(jnp.int32, (length, LANES), 0)
        return jnp.transpose(jnp.where(hit, 1.0, 0.0))[:per_dev, :].astype(BF16)

    pick = one_hot(rows_ref[...], obs_ref.shape[0])
    act_rows = [next_act_ref[...], data_act_ref[...]]
    act_rows += [samp_act_ref[i:i + 1, :] for i in range(samples)]

    def place(part):
        return [jnp.where(b == 0, part, jnp.zeros_like(part)), jnp.where(b == 0, jnp.zeros_like(part), part)]

    for j in range(cols // block):
        acts_ref[:, j * block:(j + 1) * block] = jnp.concatenate(
            place(act_rows[2 * j]) + place(act_rows[2 * j + 1]), axis=1
        )
    blank = jnp.zeros((1, states), F32)
    aux_ref[0:1, :] = jnp.concatenate([blank] + place(reward_ref[...]), axis=1)
    aux_ref[1:2, :] = jnp.concatenate([blank] + place(logp_ref[...]), axis=1)
    loads[0].wait()
    xcat[own_rows, :] = jnp.dot(pick, obs_ref[...], preferred_element_type=F32).astype(BF16)
    loads[1].wait()
    loads[2].wait()
    moved = jnp.dot(one_hot(next_act_ref[...], nact), table_ref[...], preferred_element_type=F32)
    moved = moved + jnp.dot(pick, next_ref[...], preferred_element_type=F32)
    xnext[own_rows, :] = moved.astype(BF16)
    pl.semaphore_wait(barrier, n_ens)

    def remote(src, dst, send, recv, to):
        return pltpu.make_async_remote_copy(
            src_ref=src, dst_ref=dst, send_sem=send, recv_sem=recv,
            device_id=to, device_id_type=MESH,
        )

    first = [
        remote(acts_ref, acts_in, a_send.at[0], a_recv.at[0], pair),
        remote(xcat.at[own_rows, :], xcat.at[own_rows, :], a_send.at[1], a_recv.at[1], pair),
        remote(xnext.at[own_rows, :], xnext.at[own_rows, :], a_send.at[2], a_recv.at[2], pair),
        remote(aux_ref, aux_in, a_send.at[3], a_recv.at[3], pair),
    ]
    for copy in first:
        copy.start()

    def table_step(c, carry):
        rows = pl.ds(pl.multiple_of(c * CHUNK, CHUNK), CHUNK)
        w_copy(c).wait()
        ptab[rows, :] = (0.5 * dot_t(wbuf[rows, :], table_ref[...])).astype(BF16)
        v_row = w2_ref[0:1, pl.ds(pl.multiple_of(b * half + c * CHUNK, CHUNK), CHUNK)]
        vb[rows, :] = jnp.transpose(jnp.broadcast_to(v_row, (LANES, CHUNK)))
        return carry

    lax.fori_loop(0, chunks, table_step, 0)

    first[0].wait()
    acts = acts_ref[...] + acts_in[...]
    hit = acts[:, :block] == lax.broadcasted_iota(jnp.int32, (nact, block), 0)
    picked = jnp.transpose(jnp.where(hit, 1.0, 0.0))[states:, :].astype(BF16)
    tabd[...] = jnp.dot(picked, table_ref[...], preferred_element_type=F32)
    state_row = nact + lax.rem(lax.broadcasted_iota(jnp.int32, (1, LANES), 1), states)
    for j in range(groups):
        row = lax.broadcasted_iota(jnp.int32, (nact + block, LANES), 0)
        hit = jnp.logical_or(row == acts[:, block + j * LANES:block + (j + 1) * LANES], row == state_row)
        sel[:, j * LANES:(j + 1) * LANES] = jnp.where(hit, 1.0, 0.0).astype(BF16)

    lane = lax.broadcasted_iota(jnp.int32, (1, block), 1)
    low = lane < states
    first[1].wait()
    xcat[states:, :] = (xcat[:states, :].astype(F32) + tabd[...]).astype(BF16)

    def chunk_rows(c):
        return slice(c * CHUNK, (c + 1) * CHUNK)

    def data_matmul(c):
        pcat[chunk_rows(c), :] = dot_t(wbuf[chunk_rows(c), :], xcat[...])

    def data_forward(c, q_acc):
        rows = chunk_rows(c)
        pre = pcat[rows, :]
        base[rows, :] = 0.5 * jnp.where(low, pre, pltpu.roll(pre, states, 1))
        v = vb[rows, :]
        sig = sigmoid(pre)
        silu = pre * sig
        weighted = v * (sig * (1.0 + (pre - silu)))
        lhs[rows, nact + block:] = jnp.where(low, 0.0, weighted).astype(BF16)
        cot[:, rows] = jnp.transpose(weighted)[states:, :].astype(BF16)
        return q_acc + jnp.sum(silu * v, axis=0, keepdims=True)

    q_data = jnp.zeros((1, block), F32)
    data_matmul(0)
    for c in range(chunks):
        if c + 1 < chunks:
            data_matmul(c + 1)
        q_data = data_forward(c, q_data)
    gpart[...] = jnp.dot(cot[...], wbuf[...], preferred_element_type=F32)
    gsend[...] = gpart[peer_rows, :].astype(gsend.dtype)
    qpart[:, :block] = q_data
    second = [
        remote(qpart.at[:, :block], qrecv.at[:, :block], g_send.at[0], g_recv.at[0], pair),
        remote(gsend, grecv, g_send.at[1], g_recv.at[1], pair),
        remote(qpart.at[:, block:], qrecv.at[:, block:], g_send.at[2], g_recv.at[2], pair),
    ]
    second[1].start()

    first[2].wait()

    def next_forward(c, acc):
        rows = pl.ds(pl.multiple_of(c * 2 * CHUNK, 2 * CHUNK), 2 * CHUNK)
        pre = dot_t(wbuf[rows, :], xnext[...])
        silu = pre * sigmoid(pre)
        return acc + jnp.sum(silu * vb[rows, :states], axis=0, keepdims=True)

    q_next = lax.fori_loop(0, chunks // 2, next_forward, jnp.zeros((1, states), F32))
    qpart[:, :states] = q_next
    second[0].start()

    def samp_matmul(c, buf):
        rows = pl.ds(pl.multiple_of(c * CHUNK, CHUNK), CHUNK)
        buf[...] = jnp.dot(ptab[rows, :], sel[:nact, :], preferred_element_type=F32)

    SUB = 32

    def samp_forward(c, buf, q_acc):
        q_acc = list(q_acc)
        for r in range(CHUNK // SUB):
            here = slice(r * SUB, (r + 1) * SUB)
            there = pl.ds(pl.multiple_of(c * CHUNK + r * SUB, SUB), SUB)
            v = vb[there, :]
            start = base[there, :]
            for j in range(groups):
                at = slice(j * LANES, (j + 1) * LANES)
                h = buf[here, at] + start
                t = jnp.tanh(h)
                m = h * t
                silu = h + m
                slope = (1.0 + t) * (1.0 + (h - m))
                sbuf[there, at] = slope.astype(BF16)
                ubuf[there, at] = silu.astype(BF16)
                sv = silu * v
                part = sv[0:8]
                for i in range(1, SUB // 8):
                    part = part + sv[8 * i:8 * i + 8]
                q_acc[j] = q_acc[j] + part
        return tuple(q_acc)

    def samp_pair(k, q_acc):
        samp_matmul(2 * k + 1, pbuf_b)
        q_acc = samp_forward(2 * k, pbuf_a, q_acc)
        samp_matmul(lax.rem(2 * k + 2, chunks), pbuf_a)
        return samp_forward(2 * k + 1, pbuf_b, q_acc)

    q_acc = (jnp.zeros((8, LANES), F32),) * groups
    cut_one, cut_two = chunks // 8, (chunks // 8) * 3
    samp_matmul(0, pbuf_a)
    q_acc = lax.fori_loop(0, cut_one, samp_pair, q_acc)

    def q_copy(k):
        return remote(qmine, qall.at[k], m_send.at[k], m_recv.at[k], other(k))

    def u_copy(k):
        return remote(
            usend.at[lax.rem(e + k, n_ens)], urecv.at[k], u_send.at[k], u_recv.at[k], other(k)
        )

    def s_copy(k):
        return remote(spread_mine, spread_all.at[e], s_send.at[k], s_recv.at[k], other(k))

    def start_all(make):
        def go(k, carry):
            make(k).start()
            return carry
        lax.fori_loop(1, n_ens, go, 0)

    def wait_all(make):
        def go(k, carry):
            make(k).wait()
            return carry
        lax.fori_loop(1, n_ens, go, 0)

    second[1].wait()
    grad_in = gpart[own_rows, :] + grecv[...].astype(F32)
    norm_sq = jnp.sum(grad_in * grad_in, axis=-1, keepdims=True) + 1.0
    in_norm = jnp.sqrt(norm_sq)
    unit[...] = grad_in / in_norm
    piece = usend.shape[1]
    per_col = per_dev // piece
    for p in range(n_ens):
        c0, r0 = p // per_col, (p % per_col) * piece
        usend[p] = unit[r0:r0 + piece, c0 * LANES:(c0 + 1) * LANES].astype(BF16)
    start_all(u_copy)
    second[0].wait()
    q0 = qpart[:, :block] + qrecv[:, :block]
    qmine[...] = jnp.broadcast_to(q0, qmine.shape)
    start_all(q_copy)

    q_acc = lax.fori_loop(cut_one, cut_two, samp_pair, q_acc)

    wait_all(u_copy)
    total = usend[e].astype(F32)
    for k in range(1, n_ens):
        total = total + urecv[k].astype(F32)
    spread_mine[...] = total.astype(BF16)
    spread_all[e] = total.astype(BF16)
    start_all(s_copy)
    q_acc = lax.fori_loop(cut_two, chunks // 2, samp_pair, q_acc)
    for j in range(groups):
        qpart[:, block + j * LANES:block + (j + 1) * LANES] = jnp.sum(q_acc[j], axis=0, keepdims=True)
    second[2].start()
    wait_all(q_copy)
    floor = qmine[...]
    for k in range(1, n_ens):
        floor = jnp.minimum(floor, qall[k])
    floor = pltpu.roll(floor, states, 1)[0:1, :]
    first[3].wait()
    aux = aux_ref[...] + aux_in[...]
    target = aux[0:1, :] + discount * (floor - entropy_temp * aux[1:2, :])
    td_gap = q0 - target
    dq_data = jnp.where(low, 0.0, (2.0 * td_gap - penalty_weight) / states)

    wait_all(s_copy)
    scale = 2.0 * diversity_weight / (critics_total - 1) / states
    for p in range(n_ens):
        c0, r0 = p // per_col, (p % per_col) * piece
        gpart[r0:r0 + piece, c0 * LANES:(c0 + 1) * LANES] = spread_all[p].astype(F32)
    unit_dir = unit[...]
    away = gpart[:per_dev, :] - unit_dir
    div_row = jnp.sum(unit_dir * away, axis=-1, keepdims=True)
    dg = scale * (away - unit_dir * div_row) / in_norm
    dg_rows = pl.ds(pl.multiple_of(states + b * per_dev, per_dev), per_dev)
    dgrad[:states, :] = jnp.zeros((states, width), BF16)
    dgrad[dg_rows, :] = dg.astype(BF16)
    div_sum = jnp.sum(div_row, axis=0, keepdims=True)
    div_out[...] = jnp.broadcast_to(div_sum, div_out.shape)
    third = [
        remote(dgrad.at[dg_rows, :], dgrad.at[dg_rows, :], d_send.at[0], d_recv.at[0], pair),
        remote(div_out, div_in, d_send.at[1], d_recv.at[1], pair),
    ]
    for copy in third:
        copy.start()
    second[2].wait()
    q_samp = qpart[:, block:] + qrecv[:, block:]
    exps = jnp.exp(q_samp)
    mass = exps[:, :block]
    for j in range(1, groups):
        mass = mass + exps[:, j * block:(j + 1) * block]
    mass = mass + pltpu.roll(mass, states, 1)
    log_mass = jnp.log(mass)
    tiled = jnp.concatenate([log_mass] * groups, axis=1)
    dq_samp = penalty_weight * jnp.exp(q_samp - tiled) / states
    for j in range(groups):
        at = slice(j * LANES, (j + 1) * LANES)
        sel_dq[:, at] = (sel[:, at].astype(F32) * (0.5 * dq_samp[:, at])).astype(BF16)

    def samp_gv(c, carry):
        there = pl.ds(pl.multiple_of(c * SUB * 2, SUB * 2), SUB * 2)
        total = ubuf[there, :LANES].astype(F32) * dq_samp[:, :LANES]
        for j in range(1, groups):
            at = slice(j * LANES, (j + 1) * LANES)
            total = total + ubuf[there, at].astype(F32) * dq_samp[:, at]
        gvsamp[there, :] = total
        return carry

    def samp_step(c, carry):
        rows = pl.ds(pl.multiple_of(c * 2 * CHUNK, 2 * CHUNK), 2 * CHUNK)
        grads = dot_t(sbuf[rows, :], sel_dq[...])
        v = vb[rows, :]
        for j in range((nact + block) // LANES):
            at = slice(j * LANES, (j + 1) * LANES)
            lhs[rows, at] = (v * grads[:, at]).astype(BF16)
        return carry

    lax.fori_loop(0, half // (SUB * 2), samp_gv, 0)
    steps = chunks // 2
    lax.fori_loop(0, steps // 2, samp_step, 0)
    for copy in third:
        copy.wait()
    rhs_out = [
        pltpu.make_async_copy(table_ref, rhs_hbm.at[:nact], in_sem.at[0]),
        pltpu.make_async_copy(xcat, rhs_hbm.at[nact:nact + block], in_sem.at[1]),
        pltpu.make_async_copy(dgrad, rhs_hbm.at[nact + block:], in_sem.at[2]),
    ]
    for copy in rhs_out:
        copy.start()

    def dcoef_matmul(c):
        dcoef_buf[chunk_rows(c), :] = dot_t(wbuf[chunk_rows(c), :], dgrad[...])

    def data_backward(c):
        rows = chunk_rows(c)
        dcoef = dcoef_buf[rows, :]
        pre = pcat[rows, :]
        v = vb[rows, :]
        sig = sigmoid(pre)
        silu = pre * sig
        slope = sig * (1.0 + (pre - silu))
        curve = sig * (1.0 - sig) * (2.0 + pre * (1.0 - 2.0 * sig))
        dcoef_buf[rows, :] = v * (dq_data * slope + dcoef * curve)
        gv = gvsamp[rows, :] + jnp.where(low, 0.0, dq_data * silu + dcoef * slope)
        gvbuf[b, c:c + 1, :] = jnp.sum(jnp.transpose(gv), axis=0, keepdims=True)

    dcoef_matmul(0)
    for c in range(chunks):
        if c + 1 < chunks:
            dcoef_matmul(c + 1)
        data_backward(c)
    last = remote(gvbuf.at[b], gvbuf.at[b], v_send, v_recv, pair)
    last.start()
    lax.fori_loop(steps // 2, steps, samp_step, 0)

    def lhs_copy(c):
        rows = pl.ds(c * CHUNK, CHUNK)
        return pltpu.make_async_copy(lhs.at[rows, :], lhs_hbm.at[rows, :], o_sem.at[c])

    mid = slice(nact, nact + block)
    for c in range(chunks):
        rows = chunk_rows(c)
        lhs[rows, mid] = jnp.where(low, lhs[rows, mid].astype(F32), dcoef_buf[rows, :]).astype(BF16)
        lhs_copy(c).start()

    td_total = jnp.sum(jnp.where(low, 0.0, td_gap * td_gap), axis=1, keepdims=True)
    gap_total = jnp.sum(jnp.where(low, 0.0, log_mass - q0), axis=1, keepdims=True)
    div_total = div_out[0:1, :] + div_in[0:1, :]
    stats = jnp.where(lane == 0, td_total, jnp.where(lane == 1, gap_total, div_total))
    stat_ref[...] = (stats / states)[:, :3]
    last.wait()
    for i in range(2):
        for c in range(chunks):
            at = i * half + c * CHUNK
            gv_ref[:, at:at + CHUNK] = gvbuf[i, c:c + 1, :]
    for copy in rhs_out:
        copy.wait()
    for c in range(chunks):
        lhs_copy(c).wait()


def finish(lhs_ref, rhs_ref, gv_ref, stat_ref, out_ref, gv_out, stat_out):
    out_ref[0] = jnp.dot(lhs_ref[...], rhs_ref[...], preferred_element_type=F32)

    @pl.when(pl.program_id(0) == 0)
    def small():
        gv_out[...] = gv_ref[...]
        stat_out[...] = stat_ref[...]


def body(
    replay_obs, replay_next, batch_rows, data_action, next_action, sampled_actions,
    reward, next_logp, action_table, w1, w2,
):
    per_dev = batch_rows.shape[0]
    samples = sampled_actions.shape[1]
    width = replay_obs.shape[1]
    hidden = w1.shape[1]
    n_batch = lax.axis_size("batch")
    n_ens = lax.axis_size("ens")
    if n_batch != 2 or w1.shape[0] != 1:
        raise ValueError("unsupported mesh")
    states = per_dev * n_batch
    block = 2 * states
    half = hidden // n_batch
    nact = action_table.shape[0]
    cols = (samples + 2) * states
    samp_cols = cols - block
    inner = nact + 2 * block
    chunks = half // CHUNK
    piece = per_dev * width // LANES // n_ens
    vmem = pl.BlockSpec(memory_space=pltpu.VMEM)
    anywhere = pl.BlockSpec(memory_space=pl.ANY)
    dma = pltpu.SemaphoreType.DMA
    lhs, rhs, gv, stats = pl.pallas_call(
        functools.partial(kernel, n_ens, per_dev, samples, n_ens * w1.shape[0]),
        out_shape=(
            jax.ShapeDtypeStruct((half, inner), BF16),
            jax.ShapeDtypeStruct((inner, width), BF16),
            jax.ShapeDtypeStruct((1, hidden), F32),
            jax.ShapeDtypeStruct((1, 3), F32),
        ),
        in_specs=[vmem] * 7 + [anywhere] * 4,
        out_specs=(anywhere, anywhere, vmem, vmem),
        scratch_shapes=[
            pltpu.VMEM(replay_obs.shape, BF16),
            pltpu.VMEM(replay_next.shape, BF16),
            pltpu.VMEM(action_table.shape, BF16),
            pltpu.VMEM((1, cols), jnp.int32),
            pltpu.VMEM((2, block), F32),
            pltpu.VMEM((half, width), BF16),
            pltpu.VMEM((block, width), BF16),
            pltpu.VMEM((states, width), BF16),
            pltpu.VMEM((1, cols), jnp.int32),
            pltpu.VMEM((2, block), F32),
            pltpu.VMEM((nact + block, samp_cols), BF16),
            pltpu.VMEM((nact + block, samp_cols), BF16),
            pltpu.VMEM((half, nact), BF16),
            pltpu.VMEM((CHUNK, samp_cols), F32),
            pltpu.VMEM((CHUNK, samp_cols), F32),
            pltpu.VMEM((half, block), F32),
            pltpu.VMEM((half, block), F32),
            pltpu.VMEM((half, LANES), F32),
            pltpu.VMEM((states, half), BF16),
            pltpu.VMEM((half, samp_cols), BF16),
            pltpu.VMEM((half, samp_cols), BF16),
            pltpu.VMEM((states, width), F32),
            pltpu.VMEM((per_dev, width), BF16),
            pltpu.VMEM((per_dev, width), BF16),
            pltpu.VMEM((1, cols), F32),
            pltpu.VMEM((1, cols), F32),
            pltpu.VMEM((per_dev, width), F32),
            pltpu.VMEM((n_ens, piece, LANES), BF16),
            pltpu.VMEM((n_ens, piece, LANES), BF16),
            pltpu.VMEM((8, block), F32),
            pltpu.VMEM((n_ens, 8, block), F32),
            pltpu.VMEM((piece, LANES), BF16),
            pltpu.VMEM((n_ens, piece, LANES), BF16),
            pltpu.VMEM((block, width), BF16),
            pltpu.VMEM((8, block), F32),
            pltpu.VMEM((8, block), F32),
            pltpu.VMEM((half, block), F32),
            pltpu.VMEM((half, LANES), F32),
            pltpu.VMEM((2, chunks, CHUNK), F32),
            pltpu.VMEM((half, inner), BF16),
            pltpu.VMEM((states, width), F32),
            dma((3,)), dma((chunks,)),
            dma((4,)), dma((4,)), dma((3,)), dma((3,)),
            dma((n_ens,)), dma((n_ens,)), dma((n_ens,)), dma((n_ens,)), dma((n_ens,)), dma((n_ens,)),
            dma((2,)), dma((2,)), dma, dma, dma((chunks,)),
        ],
        compiler_params=pltpu.CompilerParams(
            collective_id=0, has_side_effects=True, vmem_limit_bytes=VMEM_LIMIT
        ),
    )(
        batch_rows[None], next_action[None], data_action[None],
        sampled_actions.T, reward[None], next_logp[None], w2,
        replay_obs, replay_next, action_table, w1,
    )
    tile = half // 4
    small = pl.BlockSpec((1, hidden), lambda i: (0, 0))
    tiny = pl.BlockSpec((1, 3), lambda i: (0, 0))
    return pl.pallas_call(
        finish,
        grid=(half // tile,),
        out_shape=(
            jax.ShapeDtypeStruct((1, half, width), F32),
            jax.ShapeDtypeStruct((1, hidden), F32),
            jax.ShapeDtypeStruct((1, 3), F32),
        ),
        in_specs=[
            pl.BlockSpec((tile, inner), lambda i: (i, 0)),
            pl.BlockSpec((inner, width), lambda i: (0, 0)),
            small, tiny,
        ],
        out_specs=(pl.BlockSpec((1, tile, width), lambda i: (0, i, 0)), small, tiny),
        compiler_params=pltpu.CompilerParams(vmem_limit_bytes=VMEM_LIMIT_2),
    )(lhs, rhs, gv, stats)


def solution(mesh):
    return jax.shard_map(
        body,
        mesh=mesh,
        in_specs=(
            P("batch", None),
            P("batch", None),
            P("batch"),
            P("batch"),
            P("batch"),
            P("batch", None),
            P("batch"),
            P("batch"),
            P(),
            P("ens", None, None),
            P("ens", None),
        ),
        out_specs=(P("ens", "batch", None), P("ens", None), P("ens", None)),
        check_vma=False,
    )
```

time: 54 us -> 43.4 us (0.80)
  matrix products: 7.35 us -> 0 us
  Pallas kernels: 44.6 us -> 42.5 us
  local copies, waits for them, and re-layouts: 1.12 us -> 0 us
    pallas_call x1, Pallas kernels: 44.6 us -> 35.6 us  [body(): pl.pallas_call(functools.partial(kernel, n_ens, per_dev, samples, n_ens *...]
    dot_general x1 -> x0, matrix products: 7.35 us -> none  [body(): grad_w1 = jnp.dot(lhs, rhs, preferred_element_type=F32)[None]]
    pallas_call x0 -> x1, Pallas kernels: none -> 6.86 us  [body(): pl.pallas_call(finish, grid=(half // tile,), out_shape=(jax.ShapeDtypeStr...]
    unnamed x6 -> x0, local copies, waits for them, and re-layouts: 1.12 us -> none
where the time goes in v1:
time: 43.4 us; the launch traced here: 43.1 us
  Pallas kernels  42.5 us (98%)
  between operations  0.64 us (1%)
    pallas_call x1, Pallas kernels, body(): pl.pallas_call(functools.partial(kernel, n_ens, per_dev, samples, n_ens *...  35.6 us
    pallas_call x1, Pallas kernels, body(): pl.pallas_call(finish, grid=(half // tile,), out_shape=(jax.ShapeDtypeStr...  6.86 us

profile of v1, /device:TPU:0, one launch (start us, length us, event | category | flops | bytes accessed | tf_op | source)
XLA Modules:
  0.0 43.1 jit_solution(16922385801051969021)
XLA Ops:
  0.6 35.6 %shard_map.130 = (bf16[2048,512]{1,0:T(8,128)(2,1)}, bf16[512,1024]{1,0:T(8,128)(2,1)}, f32[1,4096]{1,0:T(1,128)}, f32[1,3]{1,0:T(1,128)}) custom-call(s32[1,32]{1,0:T(1,128)} %bitcast.7, s32[1,32]{1,0:T(1,128)} %bitcast.8, s32[1,32]{1,0:T(1,128)} %bitcast.9, s32[16,32]{1,0:T(8,128)} %bitcast.6, f32[1,32]{1,0:T(1,128)} %bitcast.10, f32[1,32]{1,0:T(1,128)} %bitcast.11, ...), custom_call_target="tpu_custom_call" | custom-call | tf_op jit(solution)/shard_map/pallas_call | solution.py:458
  36.2 6.9 %shard_map.131 = (f32[1,2048,1024]{2,1,0:T(8,128)}, f32[1,4096]{1,0:T(1,128)}, f32[1,3]{1,0:T(1,128)}) custom-call(bf16[2048,512]{1,0:T(8,128)(2,1)} %get-tuple-element.7.lhs_ref, bf16[512,1024]{1,0:T(8,128)(2,1)} %get-tuple-element.8.rhs_ref, f32[1,4096]{1,0:T(1,128)} %get-tuple-element.9.gv_ref, f32[1,3]{1,0:T(1,128)} %get-tuple-element.10.stat_ref), custom_call_target="tpu_custom_call" | custom-call | tf_op jit(solution)/shard_map/pallas_call | solution.py:526

commit v2 on v1

--- a/solution.py
+++ b/solution.py
@@ -17,8 +17,8 @@
 BF16 = jnp.bfloat16
 CHUNK = 256
 LANES = 128
-VMEM_LIMIT = 60 * 1024 * 1024
-VMEM_LIMIT_2 = 60 * 1024 * 1024
+VMEM_LIMIT = 36 * 1024 * 1024
+VMEM_LIMIT_2 = 24 * 1024 * 1024
 
 
 def dot_t(a, b):
@@ -36,10 +36,10 @@
     lhs_hbm, rhs_hbm, gv_ref, stat_ref,
     obs_ref, next_ref, table_ref, acts_ref, aux_ref, wbuf, xcat, xnext, acts_in, aux_in, sel, sel_dq, ptab,
     pbuf_a, pbuf_b, base, pcat, vb, cot, sbuf, ubuf,
-    gpart, gsend, grecv, qpart, qrecv, unit, usend, urecv, qmine, qall, spread_mine, spread_all,
-    dgrad, div_out, div_in, dcoef_buf, gvsamp, gvbuf, lhs, tabd,
+    gpart, gsend, grecv, qpart, qrecv, unit, usend, urecv, qmine, qall, spread_mine, spread_all, spread,
+    dgrad, dcoef_buf, gvsamp, gvbuf, lhs, tabd,
     in_sem, w_sem, a_send, a_recv, g_send, g_recv, u_send, u_recv, m_send, m_recv, s_send, s_recv,
-    d_send, d_recv, v_send, v_recv, o_sem,
+    v_send, v_recv, o_sem, known,
 ):
     e = lax.axis_index("ens")
     b = lax.axis_index("batch")
@@ -58,15 +58,26 @@
     def other(k):
         return {"ens": lax.rem(e + k, n_ens), "batch": b}
 
+    levels = n_ens.bit_length() - 1
+    partners = []
+    for k in range(levels):
+        step = 1 << k
+        partners.append({"ens": e + step * (1 - 2 * (lax.div(e, step) % 2)), "batch": b})
+    partners.append(pair)
     barrier = pltpu.get_barrier_semaphore()
-    pl.semaphore_signal(barrier, inc=1, device_id=pair, device_id_type=MESH)
-
-    def greet(k, carry):
-        pl.semaphore_signal(barrier, inc=1, device_id=other(k), device_id_type=MESH)
-        return carry
-
-    lax.fori_loop(1, n_ens, greet, 0)
-
+    for to in partners:
+        pl.semaphore_signal(barrier, inc=1, device_id=to, device_id_type=MESH)
+
+    def announce(k):
+        pl.semaphore_signal(known.at[k], inc=1, device_id=partners[k], device_id_type=MESH)
+
+    def advance(first_level, last_level):
+        for k in range(first_level, last_level):
+            pl.semaphore_wait(known.at[k], 1)
+            announce(k + 1)
+
+    quarter = -(-levels // 4)
+    marks = [min(levels, quarter * k) for k in range(5)]
     loads = [
         pltpu.make_async_copy(obs_hbm, obs_ref, in_sem.at[0]),
         pltpu.make_async_copy(table_hbm, table_ref, in_sem.at[1]),
@@ -81,9 +92,6 @@
             wbuf.at[pl.ds(c * CHUNK, CHUNK), :],
             w_sem.at[c],
         )
-
-    for c in range(chunks):
-        w_copy(c).start()
 
     own_rows = pl.ds(pl.multiple_of(b * per_dev, per_dev), per_dev)
     peer_rows = pl.ds(pl.multiple_of(peer * per_dev, per_dev), per_dev)
@@ -108,13 +116,11 @@
     aux_ref[0:1, :] = jnp.concatenate([blank] + place(reward_ref[...]), axis=1)
     aux_ref[1:2, :] = jnp.concatenate([blank] + place(logp_ref[...]), axis=1)
     loads[0].wait()
+    for c in range(chunks):
+        w_copy(c).start()
     xcat[own_rows, :] = jnp.dot(pick, obs_ref[...], preferred_element_type=F32).astype(BF16)
-    loads[1].wait()
-    loads[2].wait()
-    moved = jnp.dot(one_hot(next_act_ref[...], nact), table_ref[...], preferred_element_type=F32)
-    moved = moved + jnp.dot(pick, next_ref[...], preferred_element_type=F32)
-    xnext[own_rows, :] = moved.astype(BF16)
-    pl.semaphore_wait(barrier, n_ens)
+    pl.semaphore_wait(barrier, len(partners))
+    announce(0)
 
     def remote(src, dst, send, recv, to):
         return pltpu.make_async_remote_copy(
@@ -128,8 +134,16 @@
         remote(xnext.at[own_rows, :], xnext.at[own_rows, :], a_send.at[2], a_recv.at[2], pair),
         remote(aux_ref, aux_in, a_send.at[3], a_recv.at[3], pair),
     ]
-    for copy in first:
-        copy.start()
+    first[0].start()
+    first[1].start()
+    loads[1].wait()
+    moved = jnp.dot(one_hot(next_act_ref[...], nact), table_ref[...], preferred_element_type=F32)
+    loads[2].wait()
+    moved = moved + jnp.dot(pick, next_ref[...], preferred_element_type=F32)
+    xnext[own_rows, :] = moved.astype(BF16)
+    first[2].start()
+    first[3].start()
+    advance(marks[0], marks[1])
 
     def table_step(c, carry):
         rows = pl.ds(pl.multiple_of(c * CHUNK, CHUNK), CHUNK)
@@ -141,17 +155,13 @@
 
     lax.fori_loop(0, chunks, table_step, 0)
 
+    advance(marks[1], marks[2])
     first[0].wait()
     acts = acts_ref[...] + acts_in[...]
     hit = acts[:, :block] == lax.broadcasted_iota(jnp.int32, (nact, block), 0)
     picked = jnp.transpose(jnp.where(hit, 1.0, 0.0))[states:, :].astype(BF16)
     tabd[...] = jnp.dot(picked, table_ref[...], preferred_element_type=F32)
-    state_row = nact + lax.rem(lax.broadcasted_iota(jnp.int32, (1, LANES), 1), states)
-    for j in range(groups):
-        row = lax.broadcasted_iota(jnp.int32, (nact + block, LANES), 0)
-        hit = jnp.logical_or(row == acts[:, block + j * LANES:block + (j + 1) * LANES], row == state_row)
-        sel[:, j * LANES:(j + 1) * LANES] = jnp.where(hit, 1.0, 0.0).astype(BF16)
-
+    advance(marks[2], marks[3])
     lane = lax.broadcasted_iota(jnp.int32, (1, block), 1)
     low = lane < states
     first[1].wait()
@@ -182,14 +192,21 @@
             data_matmul(c + 1)
         q_data = data_forward(c, q_data)
     gpart[...] = jnp.dot(cot[...], wbuf[...], preferred_element_type=F32)
-    gsend[...] = gpart[peer_rows, :].astype(gsend.dtype)
+    gsend[...] = gpart[...].astype(BF16)
     qpart[:, :block] = q_data
     second = [
         remote(qpart.at[:, :block], qrecv.at[:, :block], g_send.at[0], g_recv.at[0], pair),
-        remote(gsend, grecv, g_send.at[1], g_recv.at[1], pair),
+        remote(gsend.at[peer_rows, :], grecv.at[peer_rows, :], g_send.at[1], g_recv.at[1], pair),
         remote(qpart.at[:, block:], qrecv.at[:, block:], g_send.at[2], g_recv.at[2], pair),
+        remote(gsend.at[own_rows, :], grecv.at[own_rows, :], g_send.at[3], g_recv.at[3], pair),
     ]
     second[1].start()
+    advance(marks[3], marks[4])
+    state_row = nact + lax.rem(lax.broadcasted_iota(jnp.int32, (1, LANES), 1), states)
+    for j in range(groups):
+        row = lax.broadcasted_iota(jnp.int32, (nact + block, LANES), 0)
+        hit = jnp.logical_or(row == acts[:, block + j * LANES:block + (j + 1) * LANES], row == state_row)
+        sel[:, j * LANES:(j + 1) * LANES] = jnp.where(hit, 1.0, 0.0).astype(BF16)
 
     first[2].wait()
 
@@ -202,6 +219,7 @@
     q_next = lax.fori_loop(0, chunks // 2, next_forward, jnp.zeros((1, states), F32))
     qpart[:, :states] = q_next
     second[0].start()
+    second[3].start()
 
     def samp_matmul(c, buf):
         rows = pl.ds(pl.multiple_of(c * CHUNK, CHUNK), CHUNK)
@@ -239,7 +257,7 @@
         return samp_forward(2 * k + 1, pbuf_b, q_acc)
 
     q_acc = (jnp.zeros((8, LANES), F32),) * groups
-    cut_one, cut_two = chunks // 8, (chunks // 8) * 3
+    cut_one = chunks // 8
     samp_matmul(0, pbuf_a)
     q_acc = lax.fori_loop(0, cut_one, samp_pair, q_acc)
 
@@ -252,25 +270,27 @@
         )
 
     def s_copy(k):
-        return remote(spread_mine, spread_all.at[e], s_send.at[k], s_recv.at[k], other(k))
-
-    def start_all(make):
+        return remote(spread_mine, spread_all.at[b, e], s_send.at[0, k], s_recv.at[0, k], other(k))
+
+    def s_cross(k):
+        to = {"ens": lax.rem(e + k, n_ens), "batch": peer}
+        return remote(spread_mine, spread_all.at[b, e], s_send.at[1, k], s_recv.at[1, k], to)
+
+    def start_all(make, begin=1):
         def go(k, carry):
             make(k).start()
             return carry
-        lax.fori_loop(1, n_ens, go, 0)
-
-    def wait_all(make):
+        lax.fori_loop(begin, n_ens, go, 0)
+
+    def wait_all(make, begin=1):
         def go(k, carry):
             make(k).wait()
             return carry
-        lax.fori_loop(1, n_ens, go, 0)
+        lax.fori_loop(begin, n_ens, go, 0)
 
     second[1].wait()
-    grad_in = gpart[own_rows, :] + grecv[...].astype(F32)
-    norm_sq = jnp.sum(grad_in * grad_in, axis=-1, keepdims=True) + 1.0
-    in_norm = jnp.sqrt(norm_sq)
-    unit[...] = grad_in / in_norm
+    grad_in = gpart[own_rows, :] + grecv[own_rows, :].astype(F32)
+    unit[...] = grad_in / jnp.sqrt(jnp.sum(grad_in * grad_in, axis=-1, keepdims=True) + 1.0)
     piece = usend.shape[1]
     per_col = per_dev // piece
     for p in range(n_ens):
@@ -282,19 +302,20 @@
     qmine[...] = jnp.broadcast_to(q0, qmine.shape)
     start_all(q_copy)
 
-    q_acc = lax.fori_loop(cut_one, cut_two, samp_pair, q_acc)
-
+    q_acc = lax.fori_loop(cut_one, chunks // 2, samp_pair, q_acc)
+    for j in range(groups):
+        qpart[:, block + j * LANES:block + (j + 1) * LANES] = jnp.sum(q_acc[j], axis=0, keepdims=True)
+    second[2].start()
+
+    pl.semaphore_wait(known.at[levels], 1)
     wait_all(u_copy)
     total = usend[e].astype(F32)
     for k in range(1, n_ens):
         total = total + urecv[k].astype(F32)
     spread_mine[...] = total.astype(BF16)
-    spread_all[e] = total.astype(BF16)
+    spread_all[b, e] = total.astype(BF16)
+    start_all(s_cross, 0)
     start_all(s_copy)
-    q_acc = lax.fori_loop(cut_two, chunks // 2, samp_pair, q_acc)
-    for j in range(groups):
-        qpart[:, block + j * LANES:block + (j + 1) * LANES] = jnp.sum(q_acc[j], axis=0, keepdims=True)
-    second[2].start()
     wait_all(q_copy)
     floor = qmine[...]
     for k in range(1, n_ens):
@@ -306,26 +327,6 @@
     td_gap = q0 - target
     dq_data = jnp.where(low, 0.0, (2.0 * td_gap - penalty_weight) / states)
 
-    wait_all(s_copy)
-    scale = 2.0 * diversity_weight / (critics_total - 1) / states
-    for p in range(n_ens):
-        c0, r0 = p // per_col, (p % per_col) * piece
-        gpart[r0:r0 + piece, c0 * LANES:(c0 + 1) * LANES] = spread_all[p].astype(F32)
-    unit_dir = unit[...]
-    away = gpart[:per_dev, :] - unit_dir
-    div_row = jnp.sum(unit_dir * away, axis=-1, keepdims=True)
-    dg = scale * (away - unit_dir * div_row) / in_norm
-    dg_rows = pl.ds(pl.multiple_of(states + b * per_dev, per_dev), per_dev)
-    dgrad[:states, :] = jnp.zeros((states, width), BF16)
-    dgrad[dg_rows, :] = dg.astype(BF16)
-    div_sum = jnp.sum(div_row, axis=0, keepdims=True)
-    div_out[...] = jnp.broadcast_to(div_sum, div_out.shape)
-    third = [
-        remote(dgrad.at[dg_rows, :], dgrad.at[dg_rows, :], d_send.at[0], d_recv.at[0], pair),
-        remote(div_out, div_in, d_send.at[1], d_recv.at[1], pair),
-    ]
-    for copy in third:
-        copy.start()
     second[2].wait()
     q_samp = qpart[:, block:] + qrecv[:, block:]
     exps = jnp.exp(q_samp)
@@ -361,8 +362,21 @@
     lax.fori_loop(0, half // (SUB * 2), samp_gv, 0)
     steps = chunks // 2
     lax.fori_loop(0, steps // 2, samp_step, 0)
-    for copy in third:
-        copy.wait()
+    second[3].wait()
+    grad_in = gpart[...] + grecv[...].astype(F32)
+    in_norm = jnp.sqrt(jnp.sum(grad_in * grad_in, axis=-1, keepdims=True) + 1.0)
+    unit_dir = grad_in / in_norm
+    wait_all(s_cross, 0)
+    wait_all(s_copy)
+    scale = 2.0 * diversity_weight / (critics_total - 1) / states
+    for i in range(2):
+        for p in range(n_ens):
+            c0, r0 = p // per_col, i * per_dev + (p % per_col) * piece
+            spread[r0:r0 + piece, c0 * LANES:(c0 + 1) * LANES] = spread_all[i, p].astype(F32)
+    away = spread[...] - unit_dir
+    div_row = jnp.sum(unit_dir * away, axis=-1, keepdims=True)
+    dgrad[:states, :] = jnp.zeros((states, width), BF16)
+    dgrad[states:, :] = (scale * (away - unit_dir * div_row) / in_norm).astype(BF16)
     rhs_out = [
         pltpu.make_async_copy(table_ref, rhs_hbm.at[:nact], in_sem.at[0]),
         pltpu.make_async_copy(xcat, rhs_hbm.at[nact:nact + block], in_sem.at[1]),
@@ -408,7 +422,7 @@
 
     td_total = jnp.sum(jnp.where(low, 0.0, td_gap * td_gap), axis=1, keepdims=True)
     gap_total = jnp.sum(jnp.where(low, 0.0, log_mass - q0), axis=1, keepdims=True)
-    div_total = div_out[0:1, :] + div_in[0:1, :]
+    div_total = jnp.sum(div_row, axis=0, keepdims=True)
     stats = jnp.where(lane == 0, td_total, jnp.where(lane == 1, gap_total, div_total))
     stat_ref[...] = (stats / states)[:, :3]
     last.wait()
@@ -422,13 +436,19 @@
         lhs_copy(c).wait()
 
 
-def finish(lhs_ref, rhs_ref, gv_ref, stat_ref, out_ref, gv_out, stat_out):
-    out_ref[0] = jnp.dot(lhs_ref[...], rhs_ref[...], preferred_element_type=F32)
-
-    @pl.when(pl.program_id(0) == 0)
-    def small():
-        gv_out[...] = gv_ref[...]
-        stat_out[...] = stat_ref[...]
+def finish(lhs_ref, rhs_ref, gv_ref, stat_ref, out_hbm, gv_out, stat_out, buf, sem):
+    gv_out[...] = gv_ref[...]
+    stat_out[...] = stat_ref[...]
+    parts = 4
+    tile = buf.shape[0] // parts
+    copies = []
+    for i in range(parts):
+        rows = pl.ds(i * tile, tile)
+        buf[rows, :] = jnp.dot(lhs_ref[rows, :], rhs_ref[...], preferred_element_type=F32)
+        copies.append(pltpu.make_async_copy(buf.at[rows, :], out_hbm.at[0, rows, :], sem.at[i]))
+        copies[-1].start()
+    for copy in copies:
+        copy.wait()
 
 
 def body(
@@ -441,7 +461,7 @@
     hidden = w1.shape[1]
     n_batch = lax.axis_size("batch")
     n_ens = lax.axis_size("ens")
-    if n_batch != 2 or w1.shape[0] != 1:
+    if n_batch != 2 or w1.shape[0] != 1 or n_ens & (n_ens - 1):
         raise ValueError("unsupported mesh")
     states = per_dev * n_batch
     block = 2 * states
@@ -454,6 +474,7 @@
     piece = per_dev * width // LANES // n_ens
     vmem = pl.BlockSpec(memory_space=pltpu.VMEM)
     anywhere = pl.BlockSpec(memory_space=pl.ANY)
+    hbm = pl.BlockSpec(memory_space=pltpu.HBM)
     dma = pltpu.SemaphoreType.DMA
     lhs, rhs, gv, stats = pl.pallas_call(
         functools.partial(kernel, n_ens, per_dev, samples, n_ens * w1.shape[0]),
@@ -463,7 +484,7 @@
             jax.ShapeDtypeStruct((1, hidden), F32),
             jax.ShapeDtypeStruct((1, 3), F32),
         ),
-        in_specs=[vmem] * 7 + [anywhere] * 4,
+        in_specs=[vmem] * 7 + [hbm] * 4,
         out_specs=(anywhere, anywhere, vmem, vmem),
         scratch_shapes=[
             pltpu.VMEM(replay_obs.shape, BF16),
@@ -488,8 +509,8 @@
             pltpu.VMEM((half, samp_cols), BF16),
             pltpu.VMEM((half, samp_cols), BF16),
             pltpu.VMEM((states, width), F32),
-            pltpu.VMEM((per_dev, width), BF16),
-            pltpu.VMEM((per_dev, width), BF16),
+            pltpu.VMEM((states, width), BF16),
+            pltpu.VMEM((states, width), BF16),
             pltpu.VMEM((1, cols), F32),
             pltpu.VMEM((1, cols), F32),
             pltpu.VMEM((per_dev, width), F32),
@@ -498,45 +519,40 @@
             pltpu.VMEM((8, block), F32),
             pltpu.VMEM((n_ens, 8, block), F32),
             pltpu.VMEM((piece, LANES), BF16),
-            pltpu.VMEM((n_ens, piece, LANES), BF16),
+            pltpu.VMEM((2, n_ens, piece, LANES), BF16),
+            pltpu.VMEM((states, width), F32),
             pltpu.VMEM((block, width), BF16),
-            pltpu.VMEM((8, block), F32),
-            pltpu.VMEM((8, block), F32),
             pltpu.VMEM((half, block), F32),
             pltpu.VMEM((half, LANES), F32),
             pltpu.VMEM((2, chunks, CHUNK), F32),
             pltpu.VMEM((half, inner), BF16),
             pltpu.VMEM((states, width), F32),
             dma((3,)), dma((chunks,)),
-            dma((4,)), dma((4,)), dma((3,)), dma((3,)),
-            dma((n_ens,)), dma((n_ens,)), dma((n_ens,)), dma((n_ens,)), dma((n_ens,)), dma((n_ens,)),
-            dma((2,)), dma((2,)), dma, dma, dma((chunks,)),
+            dma((4,)), dma((4,)), dma((4,)), dma((4,)),
+            dma((n_ens,)), dma((n_ens,)), dma((n_ens,)), dma((n_ens,)), dma((2, n_ens)), dma((2, n_ens)),
+            dma, dma, dma((chunks,)), pltpu.SemaphoreType.REGULAR((n_ens.bit_length(),)),
         ],
         compiler_params=pltpu.CompilerParams(
             collective_id=0, has_side_effects=True, vmem_limit_bytes=VMEM_LIMIT
         ),
-    )(
-        batch_rows[None], next_action[None], data_action[None],
-        sampled_actions.T, reward[None], next_logp[None], w2,
-        replay_obs, replay_next, action_table, w1,
-    )
-    tile = half // 4
-    small = pl.BlockSpec((1, hidden), lambda i: (0, 0))
-    tiny = pl.BlockSpec((1, 3), lambda i: (0, 0))
+    )(*(
+        pltpu.with_memory_space_constraint(x, pltpu.HBM)
+        for x in (
+            batch_rows[None], next_action[None], data_action[None],
+            sampled_actions.T, reward[None], next_logp[None], w2,
+            replay_obs, replay_next, action_table, w1,
+        )
+    ))
     return pl.pallas_call(
         finish,
-        grid=(half // tile,),
         out_shape=(
             jax.ShapeDtypeStruct((1, half, width), F32),
             jax.ShapeDtypeStruct((1, hidden), F32),
             jax.ShapeDtypeStruct((1, 3), F32),
         ),
-        in_specs=[
-            pl.BlockSpec((tile, inner), lambda i: (i, 0)),
-            pl.BlockSpec((inner, width), lambda i: (0, 0)),
-            small, tiny,
-        ],
-        out_specs=(pl.BlockSpec((1, tile, width), lambda i: (0, i, 0)), small, tiny),
+        in_specs=[vmem] * 4,
+        out_specs=(hbm, vmem, vmem),
+        scratch_shapes=[pltpu.VMEM((half, width), F32), dma((4,))],
         compiler_params=pltpu.CompilerParams(vmem_limit_bytes=VMEM_LIMIT_2),
     )(lhs, rhs, gv, stats)
 

time: 43.4 us -> 38.3 us (0.88)
  Pallas kernels: 42.5 us -> 37.5 us
    pallas_call x1, Pallas kernels: 35.6 us -> 32.8 us  [body(): pl.pallas_call(functools.partial(kernel, n_ens, per_dev, samples, n_ens *...]
    pallas_call x1, Pallas kernels: 6.86 us -> 4.69 us  [body(): pl.pallas_call(finish, out_shape=(jax.ShapeDtypeStruct((1, half, width),...]
where the time goes in v2:
time: 38.3 us; the launch traced here: 38.1 us
  Pallas kernels  37.5 us (98%)
  between operations  0.64 us (2%)
    pallas_call x1, Pallas kernels, body(): pl.pallas_call(functools.partial(kernel, n_ens, per_dev, samples, n_ens *...  32.8 us
    pallas_call x1, Pallas kernels, body(): pl.pallas_call(finish, out_shape=(jax.ShapeDtypeStruct((1, half, width),...  4.69 us

profile of v2, /device:TPU:0, one launch (start us, length us, event | category | flops | bytes accessed | tf_op | source)
XLA Modules:
  0.0 38.1 jit_solution(14841639338858788967)
XLA Ops:
  0.6 32.8 %shard_map.130 = (bf16[2048,512]{1,0:T(8,128)(2,1)S(1)}, bf16[512,1024]{1,0:T(8,128)(2,1)S(1)}, f32[1,4096]{1,0:T(1,128)S(1)}, f32[1,3]{1,0:T(1,128)S(1)}) custom-call(s32[1,32]{1,0:T(1,128)} %bitcast.7, s32[1,32]{1,0:T(1,128)} %bitcast.8, s32[1,32]{1,0:T(1,128)} %bitcast.9, s32[16,32]{1,0:T(8,128)} %bitcast.6, f32[1,32]{1,0:T(1,128)} %bitcast.10, ...), custom_call_target="tpu_custom_call" | custom-call | tf_op jit(solution)/shard_map/pallas_call | solution.py:479
  33.4 4.7 %shard_map.131 = (f32[1,2048,1024]{2,1,0:T(8,128)}, f32[1,4096]{1,0:T(1,128)}, f32[1,3]{1,0:T(1,128)}) custom-call(bf16[2048,512]{1,0:T(8,128)(2,1)S(1)} %get-tuple-element.7.lhs_ref, bf16[512,1024]{1,0:T(8,128)(2,1)S(1)} %get-tuple-element.8.rhs_ref, f32[1,4096]{1,0:T(1,128)S(1)} %get-tuple-element.9.gv_ref, f32[1,3]{1,0:T(1,128)S(1)} %get-tuple-element.10.stat_ref), custom_call_target="tpu_custom_call" | custom-call | tf_op jit(solution)/shard_map/pallas_call | solution.py:546

commit v3 on v2

v3 whole, which is shorter than its diff:
```python
import functools

import jax
import jax.numpy as jnp
from jax import lax
from jax.experimental import pallas as pl
from jax.experimental.pallas import tpu as pltpu
from jax.sharding import PartitionSpec as P

discount = 0.99
entropy_temp = 0.2
penalty_weight = 1.0
diversity_weight = 1000.0

MESH = pl.DeviceIdType.MESH
F32 = jnp.float32
BF16 = jnp.bfloat16
CHUNK = 256
LANES = 128
VMEM_LIMIT = 36 * 1024 * 1024
VMEM_LIMIT_2 = 24 * 1024 * 1024


def dot_t(a, b):
    return lax.dot_general(a, b, (((1,), (1,)), ((), ())), preferred_element_type=F32)


def sigmoid(x):
    return 0.5 * jnp.tanh(0.5 * x) + 0.5


def kernel(
    n_ens, per_dev, samples, critics_total,
    rows_ref, next_act_ref, data_act_ref, samp_act_ref, reward_ref, logp_ref, w2_ref,
    obs_hbm, next_hbm, table_hbm, w1_ref,
    lhs, rhs, gv_ref, stat_ref,
    obs_ref, next_ref, table_ref, acts_ref, aux_ref, wbuf, xobs, xnext, xdat, xin, xnx, acts_in, aux_in, sel, sel_dq, ptab,
    pbuf_a, pbuf_b, base, pcat, vb, cot, sbuf, ubuf,
    gpart, gsend, grecv, qpart, qrecv, unit, usend, urecv, qmine, qall, spread_mine, spread_all, spread,
    dcoef_buf, gvsamp, tabd,
    in_sem, w_sem, a_send, a_recv, g_send, g_recv, u_send, u_recv, m_send, m_recv, s_send, s_recv,
    known,
):
    e = lax.axis_index("ens")
    b = lax.axis_index("batch")
    peer = 1 - b
    states = 2 * per_dev
    block = 2 * states
    nact = table_ref.shape[0]
    width = table_ref.shape[1]
    cols = acts_ref.shape[1]
    samp_cols = cols - block
    groups = samp_cols // LANES
    half = wbuf.shape[0]
    chunks = half // CHUNK
    pairs = chunks // 2
    pair = {"ens": e, "batch": peer}

    def other(k):
        return {"ens": lax.rem(e + k, n_ens), "batch": b}

    levels = n_ens.bit_length() - 1
    cube = levels - 1
    line = n_ens // 4
    z = lax.div(e, line)
    middle = jnp.logical_and(z >= 1, z <= 2)

    def at_ens(k):
        return {"ens": k, "batch": b}

    partners = [at_ens(e + (1 << k) * (1 - 2 * (lax.div(e, 1 << k) % 2))) for k in range(cube)]
    across = at_ens(e + line * (3 - 2 * z))
    barrier = pltpu.get_barrier_semaphore()
    for to in partners + [pair]:
        pl.semaphore_signal(barrier, inc=1, device_id=to, device_id_type=MESH)

    @pl.when(middle)
    def greet_across():
        pl.semaphore_signal(barrier, inc=1, device_id=across, device_id_type=MESH)

    def tell(k, to):
        pl.semaphore_signal(known.at[k], inc=1, device_id=to, device_id_type=MESH)

    def hear(k):
        pl.semaphore_wait(known.at[k], 1)

    def advance(first_level, last_level):
        for k in range(first_level, last_level):
            hear(k)
            if k + 1 < cube:
                tell(k + 1, partners[k + 1])

    def cross_tell():
        @pl.when(middle)
        def go():
            tell(cube, across)

    def cross_hear():
        @pl.when(middle)
        def go():
            hear(cube)
            tell(cube + 1, partners[cube - 1])

    def edge_hear():
        @pl.when(jnp.logical_not(middle))
        def go():
            hear(cube + 1)

        tell(cube + 2, pair)

    third = -(-cube // 3)
    marks = [min(cube, third * k) for k in range(4)]
    loads = [
        pltpu.make_async_copy(obs_hbm, obs_ref, in_sem.at[0]),
        pltpu.make_async_copy(table_hbm, table_ref, in_sem.at[1]),
        pltpu.make_async_copy(next_hbm, next_ref, in_sem.at[2]),
    ]
    for copy in loads:
        copy.start()

    def w_copy(c):
        return pltpu.make_async_copy(
            w1_ref.at[0, pl.ds(b * half + c * CHUNK, CHUNK), :],
            wbuf.at[pl.ds(c * CHUNK, CHUNK), :],
            w_sem.at[c],
        )

    d_top = nact + 3 * states
    own_rows = pl.ds(pl.multiple_of(b * per_dev, per_dev), per_dev)
    peer_rows = pl.ds(pl.multiple_of(peer * per_dev, per_dev), per_dev)

    def one_hot(index_row, length):
        row = jnp.concatenate([index_row, jnp.zeros((1, LANES - per_dev), jnp.int32)], axis=1)
        hit = row == lax.broadcasted_iota(jnp.int32, (length, LANES), 0)
        return jnp.transpose(jnp.where(hit, 1.0, 0.0))[:per_dev, :].astype(BF16)

    pick = one_hot(rows_ref[...], obs_ref.shape[0])
    act_rows = [next_act_ref[...], data_act_ref[...]]
    act_rows += [samp_act_ref[i:i + 1, :] for i in range(samples)]

    def place(part):
        return [jnp.where(b == 0, part, jnp.zeros_like(part)), jnp.where(b == 0, jnp.zeros_like(part), part)]

    for j in range(cols // block):
        acts_ref[:, j * block:(j + 1) * block] = jnp.concatenate(
            place(act_rows[2 * j]) + place(act_rows[2 * j + 1]), axis=1
        )
    aux_ref[0:1, :] = jnp.concatenate(place(reward_ref[...]) * 2, axis=1)
    aux_ref[1:2, :] = jnp.concatenate(place(logp_ref[...]) * 2, axis=1)
    for c in range(chunks):
        w_copy(c).start()
    for g in range(pairs):
        v_row = w2_ref[0:1, pl.ds(pl.multiple_of(b * half + 2 * g * CHUNK, CHUNK), 2 * CHUNK)]
        vb[2 * g * CHUNK:2 * (g + 1) * CHUNK, :] = jnp.transpose(jnp.broadcast_to(v_row, (LANES, 2 * CHUNK)))
    for i in range(2):
        gap = slice((1 - i) * states, (2 - i) * states)
        xin[i, gap, :] = jnp.zeros((states, width), BF16)
        xnx[i, gap, :] = jnp.zeros((states, width), BF16)
        rhs[d_top + 2 * i * states:d_top + (2 * i + 1) * states, :] = jnp.zeros((states, width), BF16)
    loads[0].wait()
    xobs[own_rows, :] = jnp.dot(pick, obs_ref[...], preferred_element_type=F32).astype(BF16)
    pl.semaphore_wait(barrier, len(partners) + 1 + jnp.where(middle, 1, 0))
    tell(0, partners[0])

    def remote(src, dst, send, recv, to):
        return pltpu.make_async_remote_copy(
            src_ref=src, dst_ref=dst, send_sem=send, recv_sem=recv,
            device_id=to, device_id_type=MESH,
        )

    first = [
        remote(acts_ref, acts_in, a_send.at[0], a_recv.at[0], pair),
        remote(xobs.at[own_rows, :], xobs.at[own_rows, :], a_send.at[1], a_recv.at[1], pair),
        remote(xnext.at[own_rows, :], xnext.at[own_rows, :], a_send.at[2], a_recv.at[2], pair),
        remote(aux_ref, aux_in, a_send.at[3], a_recv.at[3], pair),
    ]
    first[0].start()
    first[1].start()
    loads[1].wait()
    moved = jnp.dot(one_hot(next_act_ref[...], nact), table_ref[...], preferred_element_type=F32)
    loads[2].wait()
    moved = moved + jnp.dot(pick, next_ref[...], preferred_element_type=F32)
    xnext[own_rows, :] = moved.astype(BF16)
    first[2].start()
    first[3].start()
    advance(marks[0], marks[1])

    for g in range(pairs):
        w_copy(2 * g).wait()
        w_copy(2 * g + 1).wait()
        rows = [slice((2 * g + i) * CHUNK, (2 * g + i + 1) * CHUNK) for i in range(2)]
        made = [dot_t(wbuf[r, :], table_ref[...]) for r in rows]
        for r, out in zip(rows, made):
            ptab[r, :] = (0.5 * out).astype(BF16)

    advance(marks[1], marks[2])
    first[0].wait()
    acts = acts_ref[...] + acts_in[...]
    hit = acts[:, :block] == lax.broadcasted_iota(jnp.int32, (nact, block), 0)
    picked = jnp.transpose(jnp.where(hit, 1.0, 0.0))[states:, :].astype(BF16)
    tabd[...] = jnp.dot(picked, table_ref[...], preferred_element_type=F32)
    advance(marks[2], marks[3])
    cross_tell()
    lane = lax.broadcasted_iota(jnp.int32, (1, block), 1)
    low = lane < states
    first[1].wait()
    obs_rows = xobs[...]
    data_rows = (obs_rows.astype(F32) + tabd[...]).astype(BF16)
    xdat[...] = data_rows
    for i in range(2):
        xin[i, i * states:(i + 1) * states, :] = data_rows
        xin[i, block:block + states, :] = obs_rows
        xin[i, block + states:, :] = obs_rows

    def chunk_rows(c):
        return slice(c * CHUNK, (c + 1) * CHUNK)

    def both(k, lhs_pair):
        one = dot_t(wbuf[chunk_rows(k), :], lhs_pair[0][...])
        two = dot_t(wbuf[chunk_rows(k + pairs), :], lhs_pair[1][...])
        return one, two

    def both_v(k):
        return jnp.where(low, vb[chunk_rows(k), :], vb[chunk_rows(k + pairs), :])

    def data_matmul(k):
        one, two = both(k, (xin.at[0], xin.at[1]))
        pcat[chunk_rows(k), :] = one[:, :block] + two[:, :block]
        base[chunk_rows(k), :] = 0.5 * one[:, block:]
        base[chunk_rows(k + pairs), :] = 0.5 * two[:, block:]

    def data_forward(k, q_acc):
        pre = pcat[chunk_rows(k), :]
        v = both_v(k)
        sig = sigmoid(pre)
        silu = pre * sig
        weighted = v * (sig * (1.0 + (pre - silu)))
        flat = jnp.transpose(weighted)
        for i in range(2):
            rows = chunk_rows(k + i * pairs)
            lhs[rows, nact + block:] = weighted.astype(BF16)
            cot[:, rows] = flat[i * states:(i + 1) * states, :].astype(BF16)
        return q_acc + jnp.sum(silu * v, axis=0, keepdims=True)

    q_data = jnp.zeros((1, block), F32)
    data_matmul(0)
    for k in range(pairs):
        if k + 1 < pairs:
            data_matmul(k + 1)
        q_data = data_forward(k, q_data)
    q_data = q_data + pltpu.roll(q_data, states, 1)
    gpart[...] = jnp.dot(cot[...], wbuf[...], preferred_element_type=F32)
    gsend[...] = gpart[...].astype(BF16)
    second = [
        remote(qpart.at[:, :block], qrecv.at[:, :block], g_send.at[0], g_recv.at[0], pair),
        remote(gsend.at[peer_rows, :], grecv.at[peer_rows, :], g_send.at[1], g_recv.at[1], pair),
        remote(qpart.at[:, block:], qrecv.at[:, block:], g_send.at[2], g_recv.at[2], pair),
        remote(gsend.at[own_rows, :], grecv.at[own_rows, :], g_send.at[3], g_recv.at[3], pair),
    ]
    second[1].start()
    cross_hear()
    row = lax.broadcasted_iota(jnp.int32, (nact + block, LANES), 0)
    own_state = lax.rem(lax.broadcasted_iota(jnp.int32, (nact + block, LANES), 1), states)
    own_state = jnp.logical_and(row >= nact, lax.rem(row - nact, states) == own_state)
    for j in range(groups):
        hit = jnp.logical_or(row == acts[:, block + j * LANES:block + (j + 1) * LANES], own_state)
        sel[:, j * LANES:(j + 1) * LANES] = jnp.where(hit, 1.0, 0.0).astype(BF16)

    rhs[:nact, :] = table_ref[...]
    rhs[nact:nact + states, :] = xdat[...]
    rhs[nact + states:nact + block, :] = xobs[...]
    rhs[nact + block:d_top, :] = xdat[...]

    first[2].wait()
    for i in range(2):
        xnx[i, i * states:(i + 1) * states, :] = xnext[...]

    def next_matmul(k):
        one, two = both(k, (xnx.at[0], xnx.at[1]))
        dcoef_buf[chunk_rows(k), :] = one + two

    q_next = jnp.zeros((1, block), F32)
    next_matmul(0)
    for k in range(pairs):
        if k + 1 < pairs:
            next_matmul(k + 1)
        pre = dcoef_buf[chunk_rows(k), :]
        q_next = q_next + jnp.sum(pre * sigmoid(pre) * both_v(k), axis=0, keepdims=True)
    q_next = q_next + pltpu.roll(q_next, states, 1)
    qpart[:, :block] = jnp.where(low, q_next, q_data)
    second[0].start()
    second[3].start()

    def samp_matmul(c, buf):
        rows = pl.ds(pl.multiple_of(c * CHUNK, CHUNK), CHUNK)
        buf[...] = jnp.dot(ptab[rows, :], sel[:nact, :], preferred_element_type=F32)

    SUB = 32

    def samp_forward(c, buf, q_acc):
        q_acc = list(q_acc)
        for r in range(CHUNK // SUB):
            here = slice(r * SUB, (r + 1) * SUB)
            there = pl.ds(pl.multiple_of(c * CHUNK + r * SUB, SUB), SUB)
            v = vb[there, :]
            start = base[there, :]
            for j in range(groups):
                at = slice(j * LANES, (j + 1) * LANES)
                h = buf[here, at] + start
                t = jnp.tanh(h)
                m = h * t
                silu = h + m
                slope = (1.0 + t) * (1.0 + (h - m))
                sbuf[there, at] = slope.astype(BF16)
                ubuf[there, at] = silu.astype(BF16)
                sv = silu * v
                part = sv[0:8]
                for i in range(1, SUB // 8):
                    part = part + sv[8 * i:8 * i + 8]
                q_acc[j] = q_acc[j] + part
        return tuple(q_acc)

    def samp_pair(k, q_acc):
        samp_matmul(2 * k + 1, pbuf_b)
        q_acc = samp_forward(2 * k, pbuf_a, q_acc)
        samp_matmul(lax.rem(2 * k + 2, chunks), pbuf_a)
        return samp_forward(2 * k + 1, pbuf_b, q_acc)

    q_acc = (jnp.zeros((8, LANES), F32),) * groups
    cut_one = chunks // 8

    def q_copy(k):
        return remote(qmine, qall.at[k], m_send.at[k], m_recv.at[k], other(k))

    def u_copy(k):
        return remote(
            usend.at[lax.rem(e + k, n_ens)], urecv.at[k], u_send.at[k], u_recv.at[k], other(k)
        )

    def s_copy(k):
        return remote(spread_mine, spread_all.at[b, e], s_send.at[0, k], s_recv.at[0, k], other(k))

    def s_cross(k):
        to = {"ens": lax.rem(e + k, n_ens), "batch": peer}
        return remote(spread_mine, spread_all.at[b, e], s_send.at[1, k], s_recv.at[1, k], to)

    def start_all(make, begin=1):
        def go(k, carry):
            make(k).start()
            return carry
        lax.fori_loop(begin, n_ens, go, 0)

    def wait_all(make, begin=1):
        def go(k, carry):
            make(k).wait()
            return carry
        lax.fori_loop(begin, n_ens, go, 0)

    second[1].wait()
    grad_in = gpart[own_rows, :] + grecv[own_rows, :].astype(F32)
    edge_hear()
    unit[...] = grad_in / jnp.sqrt(jnp.sum(grad_in * grad_in, axis=-1, keepdims=True) + 1.0)
    piece = usend.shape[1]
    per_col = per_dev // piece
    for p in range(n_ens):
        c0, r0 = p // per_col, (p % per_col) * piece
        usend[p] = unit[r0:r0 + piece, c0 * LANES:(c0 + 1) * LANES].astype(BF16)
    start_all(u_copy)
    samp_matmul(0, pbuf_a)
    q_acc = lax.fori_loop(0, cut_one, samp_pair, q_acc)
    second[0].wait()
    q0 = qpart[:, :block] + qrecv[:, :block]
    qmine[...] = jnp.broadcast_to(q0, qmine.shape)
    start_all(q_copy)

    q_acc = lax.fori_loop(cut_one, chunks // 2, samp_pair, q_acc)
    for j in range(groups):
        qpart[:, block + j * LANES:block + (j + 1) * LANES] = jnp.sum(q_acc[j], axis=0, keepdims=True)
    second[2].start()

    hear(cube + 2)
    wait_all(u_copy)
    total = usend[e].astype(F32)
    for k in range(1, n_ens):
        total = total + urecv[k].astype(F32)
    spread_mine[...] = total.astype(BF16)
    spread_all[b, e] = total.astype(BF16)
    start_all(s_cross, 0)
    start_all(s_copy)
    wait_all(q_copy)
    floor = qmine[...]
    for k in range(1, n_ens):
        floor = jnp.minimum(floor, qall[k])
    floor = floor[0:1, :]
    floor = jnp.where(low, floor, pltpu.roll(floor, states, 1))
    q_own = jnp.where(low, pltpu.roll(q0, states, 1), q0)
    first[3].wait()
    aux = aux_ref[...] + aux_in[...]
    target = aux[0:1, :] + discount * (floor - entropy_temp * aux[1:2, :])
    td_gap = q_own - target
    dq_data = (2.0 * td_gap - penalty_weight) / states

    second[2].wait()
    q_samp = qpart[:, block:] + qrecv[:, block:]
    exps = jnp.exp(q_samp)
    mass = exps[:, :block]
    for j in range(1, groups):
        mass = mass + exps[:, j * block:(j + 1) * block]
    mass = mass + pltpu.roll(mass, states, 1)
    log_mass = jnp.log(mass)
    tiled = jnp.concatenate([log_mass] * groups, axis=1)
    dq_samp = penalty_weight * jnp.exp(q_samp - tiled) / states
    for j in range(groups):
        at = slice(j * LANES, (j + 1) * LANES)
        sel_dq[:, at] = (sel[:, at].astype(F32) * (0.5 * dq_samp[:, at])).astype(BF16)

    def samp_gv(c):
        there = slice(c * LANES, (c + 1) * LANES)
        total = ubuf[there, :LANES].astype(F32) * dq_samp[:, :LANES]
        for j in range(1, groups):
            at = slice(j * LANES, (j + 1) * LANES)
            total = total + ubuf[there, at].astype(F32) * dq_samp[:, at]
        gvsamp[:, there] = jnp.sum(jnp.transpose(total), axis=0, keepdims=True)

    mid = slice(nact, nact + block)

    def samp_step(k):
        rows = slice(k * 2 * CHUNK, (k + 1) * 2 * CHUNK)
        grads = dot_t(sbuf[rows, :], sel_dq[...])
        v = vb[rows, :]
        for j in range(nact // LANES):
            at = slice(j * LANES, (j + 1) * LANES)
            lhs[rows, at] = (v * grads[:, at]).astype(BF16)
        lhs[rows, mid] = (v * grads[:, mid]).astype(BF16)

    steps = chunks // 2
    share = half // LANES // steps
    for k in range(steps):
        samp_step(k)
        for c in range(k * share, (k + 1) * share):
            samp_gv(c)
    second[3].wait()
    grad_in = gpart[...] + grecv[...].astype(F32)
    in_norm = jnp.sqrt(jnp.sum(grad_in * grad_in, axis=-1, keepdims=True) + 1.0)
    unit_dir = grad_in / in_norm
    wait_all(s_cross, 0)
    wait_all(s_copy)
    scale = 2.0 * diversity_weight / (critics_total - 1) / states
    for i in range(2):
        for p in range(n_ens):
            c0, r0 = p // per_col, i * per_dev + (p % per_col) * piece
            spread[r0:r0 + piece, c0 * LANES:(c0 + 1) * LANES] = spread_all[i, p].astype(F32)
    away = spread[...] - unit_dir
    div_row = jnp.sum(unit_dir * away, axis=-1, keepdims=True)
    dgrad_rows = (scale * (away - unit_dir * div_row) / in_norm).astype(BF16)
    rhs[d_top + states:d_top + 2 * states, :] = dgrad_rows
    shifted = (rhs.at[d_top + states:, :], rhs.at[d_top:d_top + block, :])

    def dcoef_matmul(k):
        one, two = both(k, shifted)
        dcoef_buf[chunk_rows(k), :] = one + two

    def data_backward(k):
        dcoef = dcoef_buf[chunk_rows(k), :]
        pre = pcat[chunk_rows(k), :]
        v = both_v(k)
        sig = sigmoid(pre)
        silu = pre * sig
        slope = sig * (1.0 + (pre - silu))
        curve = sig * (1.0 - sig) * (2.0 + pre * (1.0 - 2.0 * sig))
        dpre = v * (dq_data * slope + dcoef * curve)
        rows = chunk_rows(k)
        lhs[rows, mid] = jnp.where(low, dpre, lhs[rows, mid].astype(F32)).astype(BF16)
        rows = chunk_rows(k + pairs)
        lhs[rows, mid] = jnp.where(low, lhs[rows, mid].astype(F32), dpre).astype(BF16)
        flat = jnp.transpose(dq_data * silu + dcoef * slope)
        for i in range(2):
            c = k + i * pairs
            late = jnp.sum(flat[i * states:(i + 1) * states, :], axis=0, keepdims=True)
            gv_ref[:, chunk_rows(c)] = gvsamp[:, chunk_rows(c)] + late

    dcoef_matmul(0)
    for k in range(pairs):
        if k + 1 < pairs:
            dcoef_matmul(k + 1)
        data_backward(k)
    td_total = jnp.sum(jnp.where(low, td_gap * td_gap, 0.0), axis=1, keepdims=True)
    gap_total = jnp.sum(jnp.where(low, log_mass - q_own, 0.0), axis=1, keepdims=True)
    div_total = jnp.sum(div_row, axis=0, keepdims=True)
    stats = jnp.where(lane == 0, td_total, jnp.where(lane == 1, gap_total, div_total))
    stat_ref[...] = (stats / states)[:, :3]


def finish(nact, lhs_ref, rhs_ref, stat_ref, out_hbm, stat_out, buf, sem):
    stat_out[...] = stat_ref[...]
    parts = sem.shape[0]
    tile = buf.shape[0] // parts
    states = (lhs_ref.shape[1] - nact) // 4
    block = 2 * states
    mids = []
    for i in range(2):
        x_top = nact + i * states
        d_top = nact + block + (2 - i) * states
        mids.append(jnp.concatenate([rhs_ref[x_top:x_top + block, :], rhs_ref[d_top:d_top + block, :]], axis=0))
    copies = []
    for i in range(parts):
        rows = pl.ds(i * tile, tile)
        out = jnp.dot(lhs_ref[rows, :nact], rhs_ref[:nact, :], preferred_element_type=F32)
        out += jnp.dot(lhs_ref[rows, nact:], mids[2 * i // parts], preferred_element_type=F32)
        buf[rows, :] = out
        copies.append(pltpu.make_async_copy(buf.at[rows, :], out_hbm.at[0, rows, :], sem.at[i]))
        copies[-1].start()
    for copy in copies:
        copy.wait()


def body(
    replay_obs, replay_next, batch_rows, data_action, next_action, sampled_actions,
    reward, next_logp, action_table, w1, w2,
):
    per_dev = batch_rows.shape[0]
    samples = sampled_actions.shape[1]
    width = replay_obs.shape[1]
    hidden = w1.shape[1]
    n_batch = lax.axis_size("batch")
    n_ens = lax.axis_size("ens")
    if n_batch != 2 or w1.shape[0] != 1 or n_ens & (n_ens - 1) or n_ens < 8:
        raise ValueError("unsupported mesh")
    states = per_dev * n_batch
    block = 2 * states
    half = hidden // n_batch
    nact = action_table.shape[0]
    cols = (samples + 2) * states
    samp_cols = cols - block
    inner = nact + 2 * block
    chunks = half // CHUNK
    piece = per_dev * width // LANES // n_ens
    vmem = pl.BlockSpec(memory_space=pltpu.VMEM)
    anywhere = pl.BlockSpec(memory_space=pl.ANY)
    hbm = pl.BlockSpec(memory_space=pltpu.HBM)
    dma = pltpu.SemaphoreType.DMA
    lhs, rhs, gv, stats = pl.pallas_call(
        functools.partial(kernel, n_ens, per_dev, samples, n_ens * w1.shape[0]),
        out_shape=(
            pltpu.VMEM((half, inner), BF16),
            pltpu.VMEM((nact + 6 * states, width), BF16),
            jax.ShapeDtypeStruct((1, half), F32),
            jax.ShapeDtypeStruct((1, 3), F32),
        ),
        in_specs=[vmem] * 7 + [hbm] * 4,
        out_specs=(vmem,) * 4,
        scratch_shapes=[
            pltpu.VMEM(replay_obs.shape, BF16),
            pltpu.VMEM(replay_next.shape, BF16),
            pltpu.VMEM(action_table.shape, BF16),
            pltpu.VMEM((1, cols), jnp.int32),
            pltpu.VMEM((2, block), F32),
            pltpu.VMEM((half, width), BF16),
            pltpu.VMEM((states, width), BF16),
            pltpu.VMEM((states, width), BF16),
            pltpu.VMEM((states, width), BF16),
            pltpu.VMEM((2, 2 * block, width), BF16),
            pltpu.VMEM((2, block, width), BF16),
            pltpu.VMEM((1, cols), jnp.int32),
            pltpu.VMEM((2, block), F32),
            pltpu.VMEM((nact + block, samp_cols), BF16),
            pltpu.VMEM((nact + block, samp_cols), BF16),
            pltpu.VMEM((half, nact), BF16),
            pltpu.VMEM((CHUNK, samp_cols), F32),
            pltpu.VMEM((CHUNK, samp_cols), F32),
            pltpu.VMEM((half, block), F32),
            pltpu.VMEM((half // 2, block), F32),
            pltpu.VMEM((half, LANES), F32),
            pltpu.VMEM((states, half), BF16),
            pltpu.VMEM((half, samp_cols), BF16),
            pltpu.VMEM((half, samp_cols), BF16),
            pltpu.VMEM((states, width), F32),
            pltpu.VMEM((states, width), BF16),
            pltpu.VMEM((states, width), BF16),
            pltpu.VMEM((1, cols), F32),
            pltpu.VMEM((1, cols), F32),
            pltpu.VMEM((per_dev, width), F32),
            pltpu.VMEM((n_ens, piece, LANES), BF16),
            pltpu.VMEM((n_ens, piece, LANES), BF16),
            pltpu.VMEM((8, block), F32),
            pltpu.VMEM((n_ens, 8, block), F32),
            pltpu.VMEM((piece, LANES), BF16),
            pltpu.VMEM((2, n_ens, piece, LANES), BF16),
            pltpu.VMEM((states, width), F32),
            pltpu.VMEM((half // 2, block), F32),
            pltpu.VMEM((1, half), F32),
            pltpu.VMEM((states, width), F32),
            dma((3,)), dma((chunks,)),
            dma((4,)), dma((4,)), dma((4,)), dma((4,)),
            dma((n_ens,)), dma((n_ens,)), dma((n_ens,)), dma((n_ens,)), dma((2, n_ens)), dma((2, n_ens)),
            pltpu.SemaphoreType.REGULAR((n_ens.bit_length() + 1,)),
        ],
        compiler_params=pltpu.CompilerParams(
            collective_id=0, has_side_effects=True, vmem_limit_bytes=VMEM_LIMIT
        ),
    )(*(
        pltpu.with_memory_space_constraint(x, pltpu.HBM)
        for x in (
            batch_rows[None], next_action[None], data_action[None],
            sampled_actions.T, reward[None], next_logp[None], w2,
            replay_obs, replay_next, action_table, w1,
        )
    ))
    swapped = lax.ppermute(gv, "batch", [(0, 1), (1, 0)])
    first = lax.axis_index("batch") == 0
    grad_w2 = jnp.concatenate(
        [jnp.where(first, gv, swapped), jnp.where(first, swapped, gv)], axis=1
    )
    grad_w1, stats = pl.pallas_call(
        functools.partial(finish, nact),
        out_shape=(
            jax.ShapeDtypeStruct((1, half, width), F32),
            jax.ShapeDtypeStruct((1, 3), F32),
        ),
        in_specs=[vmem] * 3,
        out_specs=(hbm, vmem),
        scratch_shapes=[pltpu.VMEM((half, width), F32), dma((4,))],
        compiler_params=pltpu.CompilerParams(vmem_limit_bytes=VMEM_LIMIT_2),
        cost_estimate=pl.CostEstimate(
            flops=2 * half * width * inner, bytes_accessed=4 * half * width, transcendentals=0
        ),
    )(lhs, rhs, stats)
    return grad_w1, grad_w2, stats


def solution(mesh):
    return jax.shard_map(
        body,
        mesh=mesh,
        in_specs=(
            P("batch", None),
            P("batch", None),
            P("batch"),
            P("batch"),
            P("batch"),
            P("batch", None),
            P("batch"),
            P("batch"),
            P(),
            P("ens", None, None),
            P("ens", None),
        ),
        out_specs=(P("ens", "batch", None), P("ens", None), P("ens", None)),
        check_vma=False,
    )
```

time: 38.3 us -> 37.5 us (0.979)
  Pallas kernels: 37.5 us -> 34.9 us
  starting transfers between devices: 0 us -> 1 us
  other arithmetic: 0 us -> 0.64 us
    pallas_call x1, Pallas kernels: 32.8 us -> 30.4 us  [body(): pl.pallas_call(functools.partial(kernel, n_ens, per_dev, samples, n_ens *...]
    ppermute x0 -> x1, starting transfers between devices: none -> 1 us  [body(): swapped = lax.ppermute(gv, 'batch', [(0, 1), (1, 0)])]
    concatenate x0 -> x1, other arithmetic: none -> 0.62 us  [body(): jnp.concatenate([jnp.where(first, gv, swapped), jnp.where(first, swapped,...]
  transfers between devices with their start and end apart: 0 -> 1, of which waited for: 0 -> 0; matrix products, arithmetic and copies ran while one was open for 0% -> 0% of each run, Pallas kernels for 0% -> 12%
where the time goes in v3:
time: 37.5 us; the launch traced here: 37.3 us
  Pallas kernels  34.9 us (93%)
  starting transfers between devices  1 us (3%)
  between operations  0.67 us (2%)
  other arithmetic  0.64 us (2%)
    pallas_call x1, Pallas kernels, body(): pl.pallas_call(functools.partial(kernel, n_ens, per_dev, samples, n_ens *...  30.4 us
    pallas_call x1, Pallas kernels, body(): pl.pallas_call(functools.partial(finish, nact), out_shape=(jax.ShapeDtype...  4.58 us
    ppermute x1, starting transfers between devices, body(): swapped = lax.ppermute(gv, 'batch', [(0, 1), (1, 0)])  1 us
  transfers between devices with their start and end apart: 1, of which 0 were waited for; matrix products, arithmetic and copies ran while one was open for 0% of the time, Pallas kernels for 12%

profile of v3, /device:TPU:0, one launch (start us, length us, event | category | flops | bytes accessed | tf_op | source)
XLA Modules:
  0.0 37.3 jit_solution(6863937264310939489)
XLA Ops:
  0.6 30.4 %shard_map.130 = (bf16[2048,512]{1,0:T(8,128)(2,1)S(1)}, bf16[640,1024]{1,0:T(8,128)(2,1)S(1)}, f32[1,2048]{1,0:T(1,128)S(1)}, f32[1,3]{1,0:T(1,128)S(1)}) custom-call(s32[1,32]{1,0:T(1,128)} %bitcast.7, s32[1,32]{1,0:T(1,128)} %bitcast.8, s32[1,32]{1,0:T(1,128)} %bitcast.9, s32[16,32]{1,0:T(8,128)} %bitcast.6, f32[1,32]{1,0:T(1,128)} %bitcast.10, ...), custom_call_target="tpu_custom_call" | custom-call | tf_op jit(solution)/shard_map/pallas_call | solution.py:542
  31.0 1.0 %collective-permute-start = (f32[1,2048]{1,0:T(1,128)S(1)}, f32[1,2048]{1,0:T(1,128)S(1)}, u32[]{:S(2)}, u32[]{:S(2)}) collective-permute-start(f32[1,2048]{1,0:T(1,128)S(1)} %get-tuple-element.13), channel_id=1, source_target_pairs={{0,1},{1,0},{2,3},{3,2},{4,5},{5,4},{6,7},{7,6},{8,9},{9,8},{10,11... | collective-permute-start | bytes 24584 | tf_op jit(solution)/shard_map/ppermute | solution.py:609
  32.0 4.6 %shard_map.131 = (f32[1,2048,1024]{2,1,0:T(8,128)}, f32[1,3]{1,0:T(1,128)}) custom-call(bf16[2048,512]{1,0:T(8,128)(2,1)S(1)} %get-tuple-element.9.lhs_ref, bf16[640,1024]{1,0:T(8,128)(2,1)S(1)} %get-tuple-element.10.rhs_ref, f32[1,3]{1,0:T(1,128)S(1)} %get-tuple-element.11.stat_ref), custom_call_target="tpu_custom_call" | custom-call | flops 2147483648 | bytes 8388608 | tf_op jit(solution)/shard_map/pallas_call | solution.py:614
  36.6 0.0 collective-permute-done
  36.6 0.6 %pad_maximum_fusion = f32[1,4096]{1,0:T(1,128)} fusion(f32[1,2048]{1,0:T(1,128)S(1)} %get-tuple-element.16, f32[1,2048]{1,0:T(1,128)S(1)} %get-tuple-element.15), kind=kLoop, calls=%fused_computation | loop fusion | flops 4096 | bytes 32768 | tf_op jit(solution)/shard_map/concatenate | solution.py:611
  (1 shorter events, 0.0 us)
Async XLA Ops:
  31.0 5.6 %collective-permute-start = (f32[1,2048]{1,0:T(1,128)S(1)}, f32[1,2048]{1,0:T(1,128)S(1)}, u32[]{:S(2)}, u32[]{:S(2)}) collective-permute-start(f32[1,2048]{1,0:T(1,128)S(1)} %get-tuple-element.13), channel_id=1, source_target_pairs={{0,1},{1,0},{2,3},{3,2},{4,5},{5,4},{6,7},{7,6},{8,9},{9,8},{10,11... | collective-permute-start | bytes 24584 | tf_op jit(solution)/shard_map/ppermute | solution.py:609
